TPU v7x, 256 devices: a 8x8x2 block of a 8x8x16 slice. The times are simulated.
256 devices in a mesh: groups: 2 (over z), section: 2 (over core), expert: 64 (over y, x).
Axes of the slice: x: 8, y: 8, z: 2, core: 2. Of those that a mesh axis runs over, the one named last changes fastest.
The devices are a block of a 8x8x16 slice.
Arguments:
- tokens: bfloat16 [2, 1024, 6144], P(None, ('groups', 'expert')), parts along dimension 1, may hold values from -6 to 6
- expert_ids: int32 [2, 2, 1024, 2], P('section', None, ('groups', 'expert')), parts along dimension 2, may hold values from 0 to 7, all different within a row; in each aligned block of 8 rows (0 to 7, 8 to 15, ..., all dimensions but the last counted through in order) at most 4 rows name the same one
- norm_gain: bfloat16 [2, 6144], P('section'), may hold values from 0.25 to 1.75
- router: bfloat16 [2, 6144, 8], P('section'), may hold values from -0.078125 to 0.078125
- w_gate: bfloat16 [2, 6144, 16384], P('section', None, 'expert'), may hold values from -0.078125 to 0.078125
- w_up: bfloat16 [2, 6144, 16384], P('section', None, 'expert'), may hold values from -0.078125 to 0.078125
- w_down: bfloat16 [2, 16384, 6144], P('section', 'expert'), may hold values from -0.0625 to 0.0625
Outputs:
- mixed: bfloat16 [2, 1024, 6144], P('section', ('groups', 'expert')), parts along dimension 1
There are 2 independent parts, one for each index of `groups`. A program takes and returns all parts, laid end to end along the dimension named above; an argument that names none is the same for every part. Nothing has to cross between parts.
Inputs may be any that keep to these rules, and one draw needn't show every extreme that they name: `expert_ids`: in each aligned block of 8 rows (one index of expert, one micro-batch, one layer) no expert is named by more than 4 of the pairs; a token's two ids differ.
All inputs are finite; a program needn't handle non-finite values.
Results may differ from a plain program's by a relative error of at most 0.0055.
Values may be sent and summed in bfloat16 or wider, within the bound.
A program may use at most 128 MiB of HBM per device.

v0:
```python
import jax
import jax.numpy as jnp
from jax import lax
from jax.sharding import PartitionSpec as P

D = 6144
NEXP = 8
TOPK = 2
E_WIN = 2
CAP = 4


epsilon = 1e-05


def side_by_side(arrays, axis, dim, along):
    ends, at = ([], 0)
    for a in arrays[:-1]:
        at += a.shape[along]
        ends.append(at)
    both = jnp.concatenate(arrays, axis=along)
    return tuple(jnp.split(lax.all_gather(both, axis, axis=dim, tiled=True), ends, axis=along))


def as_sent(shard):

    def short(part):
        return part.astype(jnp.bfloat16) if part.dtype == jnp.float32 else part

    return jax.tree.map(short, shard)


def shifted(value, axis, steps):
    count = lax.axis_size(axis)
    pairs = [(source, (source + steps) % count) for source in range(count)]
    return lax.ppermute(value, axis, pairs)


def normalize(stream, gain):
    values = stream.astype(jnp.float32)
    scale = lax.rsqrt(jnp.mean(values * values, axis=-1, keepdims=True) + epsilon)
    return (values * scale * gain.astype(jnp.float32)).astype(jnp.bfloat16)


def route(normed, chosen_ids, router_matrix):
    logits = jnp.dot(normed, router_matrix, preferred_element_type=jnp.float32)
    chosen_hot = (chosen_ids[..., None] == jnp.arange(NEXP, dtype=jnp.int32)).astype(jnp.float32)
    chosen = jnp.sum(chosen_hot * logits[:, None, :], axis=-1)
    first = jax.nn.sigmoid(chosen[:, 0] - chosen[:, 1])
    second = jax.nn.sigmoid(chosen[:, 1] - chosen[:, 0])
    gates = jnp.stack([first, second], axis=1)
    flat = chosen_hot.reshape(-1, NEXP)
    before = jnp.cumsum(flat, axis=0) - flat
    position = jnp.sum(before * flat, axis=-1)
    slot_hot = (position[:, None] == jnp.arange(CAP, dtype=jnp.float32)).astype(jnp.float32)
    assign = (flat[:, :E_WIN, None] * slot_hot[:, None, :]).reshape(-1, TOPK, E_WIN * CAP)
    pick = jnp.sum(assign, axis=1)
    weights = jnp.sum(gates[:, :, None] * assign, axis=1)
    return (pick, weights)


def body(tokens, expert_ids, norm_gain, router, w_gate, w_up, w_down):
    devices = lax.axis_size("expert")
    split = devices // E_WIN
    my_expert = lax.axis_index("expert") // split
    section_index = lax.axis_index("section")
    own_params = (w_gate[0], w_up[0], w_down[0], norm_gain[0], router[0])
    own_block = own_params + (expert_ids[0].astype(jnp.bfloat16),)
    other_block = jax.tree.map(
        lambda part, own: part.astype(own.dtype),
        shifted(as_sent(own_block), "section", 1),
        own_block,
    )
    stream = lax.dynamic_index_in_dim(tokens, section_index, 0, keepdims=False)
    for order_index in range(2):
        if order_index == 0:
            use_own = section_index == 0
        else:
            use_own = section_index != 0
        chosen_block = jax.tree.map(
            lambda mine_part, other_part: jnp.where(use_own, mine_part, other_part),
            own_block,
            other_block,
        )
        chosen_ids = lax.dynamic_index_in_dim(
            chosen_block[5], section_index, 0, keepdims=False
        ).astype(jnp.int32)
        gate_matrix, up_matrix, down_matrix, gain, router_matrix = chosen_block[:5]
        normed = normalize(stream, gain)
        pick, weights = route(normed, chosen_ids, router_matrix)
        pick_half = pick.astype(jnp.bfloat16)
        all_normed, all_pick = side_by_side((normed, pick_half), "expert", 0, 1)
        mine = lax.dynamic_slice_in_dim(all_pick, my_expert * CAP, CAP, 1)
        gathered = jnp.einsum(
            "stc,std->scd",
            mine.reshape(devices, -1, CAP),
            all_normed.reshape(devices, -1, D),
            preferred_element_type=jnp.float32,
        ).astype(jnp.bfloat16)
        sources, count, width = gathered.shape
        flat_rows = gathered.reshape(sources * count, width)
        gate_value = jnp.dot(flat_rows, gate_matrix, preferred_element_type=jnp.float32)
        up_value = jnp.dot(flat_rows, up_matrix, preferred_element_type=jnp.float32)
        hidden = (jax.nn.silu(gate_value) * up_value).astype(jnp.bfloat16)
        term = jnp.dot(hidden, down_matrix, preferred_element_type=jnp.float32).astype(jnp.bfloat16)
        terms = term.reshape(sources, count, width)
        returned = lax.all_to_all(terms, "expert", split_axis=0, concat_axis=0, tiled=True)
        expert_out = jnp.sum(returned.reshape(E_WIN, split, CAP, D).astype(jnp.float32), axis=1)
        moe = jnp.dot(weights, expert_out.reshape(E_WIN * CAP, D), precision=lax.Precision.HIGHEST)
        stream = (stream.astype(jnp.float32) + moe).astype(jnp.bfloat16)
    return stream[None]


def solution(mesh):
    in_specs = (
        P(None, ("groups", "expert"), None),
        P("section", None, ("groups", "expert"), None),
        P("section", None),
        P("section", None, None),
        P("section", None, "expert"),
        P("section", None, "expert"),
        P("section", "expert", None),
    )
    out_specs = P("section", ("groups", "expert"), None)
    return jax.shard_map(body, mesh=mesh, in_specs=in_specs, out_specs=out_specs, check_vma=False)
```

profile of v0, /device:TPU:514, one launch (start us, length us, event | category | flops | bytes accessed | tf_op | source)
XLA Modules:
  0.0 439.5 jit_solution(2380108209334688910)
XLA Ops:
  8.8 1.1 fusion.20
  11.3 1.0 fusion.22
  12.3 1.1 fusion.31
  15.4 104.7 %all-gather.3.cloned.1.call-done = bf16[512,6152]{1,0:T(8,128)(2,1)} async-done(((bf16[8,6152]{1,0:T(8,128)(2,1)}), bf16[512,6152]{1,0:T(8,128)(2,1)}) %all-gather.3.cloned.1.call-update) | async-done | bytes 6299664 | tf_op jit(solution)/shard_map/all_gather | solution.py:22
  121.1 5.9 %convolution_convert_fusion.3 = bf16[64,4,6144]{2,1,0:T(4,128)(2,1)S(1)} fusion(bf16[512,6152]{1,0:T(8,128)(2,1)} %all-gather.3.cloned.1.call-done, bf16[512,8]{1,0:T(8,128)(2,1)S(1)} %split.16, s32[]{:T(128)S(6)} %select_n.102), kind=kOutput, calls=%fused_computation.3 | convolution fusion | flops 26738688 | bytes 9445380 | tf_op jit(solution)/shard_map/stc,std->scd/dot_general | solution.py:94
  127.0 2.4 reshape.135
  129.4 4.0 fusion.10
  134.1 1.1 fusion.12
  135.5 1.1 convolution_convert_fusion.2
  136.5 2.7 reshape.136
  139.2 9.7 %all-to-all-start = ((bf16[64,4,6144]{2,1,0:T(4,128)(2,1)}), bf16[64,4,6144]{2,1,0:T(4,128)(2,1)S(1)}, u32[]{:S(2)}, u32[]{:S(2)}) async-start(bf16[64,4,6144]{2,1,0:T(4,128)(2,1)} %reshape.136), calls=%async_computation | async-start | bytes 6291456 | tf_op jit(solution)/shard_map/all_to_all | solution.py:107
  149.9 71.0 %all-to-all-done = bf16[64,4,6144]{2,1,0:T(4,128)(2,1)S(1)} async-done(((bf16[64,4,6144]{2,1,0:T(4,128)(2,1)}), bf16[64,4,6144]{2,1,0:T(4,128)(2,1)S(1)}, u32[]{:S(2)}, u32[]{:S(2)}) %all-to-all-start) | async-done | bytes 3145760 | tf_op jit(solution)/shard_map/all_to_all | solution.py:107
  220.9 1.4 convert_reduce_fusion.1
  223.7 1.1 fusion.29
  225.9 101.2 %all-gather.5.cloned.1.call-done = bf16[512,6152]{1,0:T(8,128)(2,1)} async-done(((bf16[8,6152]{1,0:T(8,128)(2,1)}), bf16[512,6152]{1,0:T(8,128)(2,1)}) %all-gather.5.cloned.1.call-update) | async-done | bytes 6299664 | tf_op jit(solution)/shard_map/all_gather | solution.py:22
  328.0 5.9 %convolution_convert_fusion.1 = bf16[64,4,6144]{2,1,0:T(4,128)(2,1)S(1)} fusion(bf16[512,6152]{1,0:T(8,128)(2,1)} %all-gather.5.cloned.1.call-done, bf16[512,8]{1,0:T(8,128)(2,1)S(1)} %split.18, s32[]{:T(128)S(6)} %select_n.102), kind=kOutput, calls=%fused_computation.1 | convolution fusion | flops 26738688 | bytes 9445380 | tf_op jit(solution)/shard_map/stc,std->scd/dot_general | solution.py:94
  333.9 2.4 reshape.140
  336.3 4.9 %fusion.5 = f32[256,256]{1,0:T(8,128)S(1)} fusion(bf16[256,6144]{1,0:T(8,128)(2,1)} %reshape.140, bf16[6144,256]{1,0:T(8,128)(2,1)} %collective-permute-done.4, pred[]{:T(512)S(6)} %ne.13, bf16[1,6144,256]{2,1,0:T(8,128)(2,1)} %param.12), kind=kOutput, calls=%fused_computation.15 | convolution fusion | flops 806879232 | bytes 9699329 | tf_op jit(solution)/shard_map/dot_general | solution.py:103
  341.9 3.2 fusion.7
  345.1 3.0 convolution_convert_fusion
  348.1 2.7 reshape.141
  350.8 79.5 %all_to_all.10 = bf16[64,4,6144]{2,1,0:T(4,128)(2,1)S(1)} all-to-all(bf16[64,4,6144]{2,1,0:T(4,128)(2,1)} %reshape.141), channel_id=1, replica_groups=mesh['groups'=2,'section'=2,'expert'=64] {'expert'}, dimensions={0} | all-to-all | bytes 6291456 | tf_op jit(solution)/shard_map/all_to_all | solution.py:107
  430.2 1.4 convert_reduce_fusion
  431.7 1.0 fusion.3
  (72 shorter events, 12.6 us)
Async XLA Ops:
  6.5 113.6 %all-gather.3.cloned.1.call-start = ((), (), s32[]{:S(2)}) async-start(), calls=%async_computation.2 | async-start | bytes 6522880 | tf_op jit(solution)/shard_map/all_gather | solution.py:22
  7.2 2.7 collective-permute-start
  8.0 2.6 collective-permute-start.1
  8.7 3.6 collective-permute-start.2
  12.2 107.9 %copy-start.5 = (bf16[6144,8]{0,1:T(8,128)(2,1)}, bf16[6144,8]{0,1:T(8,128)(2,1)S(1)}, u32[]{:S(2)}) copy-start(bf16[6144,8]{0,1:T(8,128)(2,1)S(1)} %collective-permute-done.2) | copy-start | bytes 294916
  14.4 115.0 %collective-permute-start.4 = (bf16[6144,256]{1,0:T(8,128)(2,1)}, bf16[6144,256]{1,0:T(8,128)(2,1)}, u32[]{:S(2)}, u32[]{:S(2)}) collective-permute-start(bf16[6144,256]{1,0:T(8,128)(2,1)} %bitcast.83), channel_id=1, source_target_pairs={{0,64},{64,0},{1,65},{65,1},{2,66},{66,2},{3,67},{67,3},{4,68},{68... | collective-permute-start | bytes 9437192 | tf_op jit(solution)/shard_map/ppermute | solution.py:36
  14.9 118.5 %collective-permute-start.3 = (bf16[6144,256]{1,0:T(8,128)(2,1)}, bf16[6144,256]{1,0:T(8,128)(2,1)}, u32[]{:S(2)}, u32[]{:S(2)}) collective-permute-start(bf16[6144,256]{1,0:T(8,128)(2,1)} %bitcast.84), channel_id=1, source_target_pairs={{0,64},{64,0},{1,65},{65,1},{2,66},{66,2},{3,67},{67,3},{4,68},{68... | collective-permute-start | bytes 9437192 | tf_op jit(solution)/shard_map/ppermute | solution.py:36
  15.1 120.2 %collective-permute-start.5 = (bf16[256,6144]{1,0:T(8,128)(2,1)}, bf16[256,6144]{1,0:T(8,128)(2,1)}, u32[]{:S(2)}, u32[]{:S(2)}) collective-permute-start(bf16[256,6144]{1,0:T(8,128)(2,1)} %bitcast.77), channel_id=1, source_target_pairs={{0,64},{64,0},{1,65},{65,1},{2,66},{66,2},{3,67},{67,3},{4,68},{68... | collective-permute-start | bytes 9437192 | tf_op jit(solution)/shard_map/ppermute | solution.py:36
  129.4 4.0 copy-start.2
  129.4 4.7 %copy-start.6 = (bf16[1,6144,256]{2,1,0:T(8,128)(2,1)S(1)}, bf16[1,6144,256]{2,1,0:T(8,128)(2,1)}, u32[]{:S(2)}) copy-start(bf16[1,6144,256]{2,1,0:T(8,128)(2,1)} %param.11) | copy-start | bytes 9437188
  133.4 2.1 copy-start
  139.2 81.7 %all-to-all-start = ((bf16[64,4,6144]{2,1,0:T(4,128)(2,1)}), bf16[64,4,6144]{2,1,0:T(4,128)(2,1)S(1)}, u32[]{:S(2)}, u32[]{:S(2)}) async-start(bf16[64,4,6144]{2,1,0:T(4,128)(2,1)} %reshape.136), calls=%async_computation | async-start | bytes 6291456 | tf_op jit(solution)/shard_map/all_to_all | solution.py:107
  148.9 73.5 %copy-start.4 = (bf16[2,8,6144]{2,1,0:T(8,128)(2,1)S(1)}, bf16[2,8,6144]{2,1,0:T(8,128)(2,1)}, u32[]{:S(2)}) copy-start(bf16[2,8,6144]{2,1,0:T(8,128)(2,1)} %param.7) | copy-start | bytes 589828
  149.0 178.2 %all-gather.5.cloned.1.call-start = ((), (), s32[]{:S(2)}) async-start(), calls=%async_computation.3 | async-start | bytes 6522880 | tf_op jit(solution)/shard_map/all_gather | solution.py:22
  336.3 4.9 %copy-start.3 = (bf16[256,6144]{1,0:T(8,128)(2,1)S(1)}, bf16[256,6144]{1,0:T(8,128)(2,1)}, u32[]{:S(2)}) copy-start(bf16[256,6144]{1,0:T(8,128)(2,1)} %reshape.140) | copy-start | bytes 9437188
  336.3 5.6 %copy-start.7 = (bf16[1,6144,256]{2,1,0:T(8,128)(2,1)S(1)}, bf16[1,6144,256]{2,1,0:T(8,128)(2,1)}, u32[]{:S(2)}) copy-start(bf16[1,6144,256]{2,1,0:T(8,128)(2,1)} %param.11) | copy-start | bytes 9437188
  341.9 3.2 copy-start.1
Sparse Core Ops, SparseCore 0:
  14.6 105.5 all-gather.2
  226.0 101.0 all-gather.4
where the time goes:
time: 441 us; the launch traced here: 440 us
  waiting for transfers between devices  277 us (63%)
  blocking collectives  79.5 us (18%)
  matrix products  32.5 us (7%)
  local copies, waits for them, and re-layouts  14.5 us (3%)
  between operations  13.7 us (3%)
  starting transfers between devices  11.7 us (3%)
  other arithmetic  10.6 us (2%)
    all_gather x2, waiting for transfers between devices, side_by_side(): lax.all_gather(both, axis, axis=dim, tiled=True)  206 us
    all_to_all x1, blocking collectives, body(): lax.all_to_all(terms, 'expert', split_axis=0, concat_axis=0, tiled=True)  79.5 us
    all_to_all x1, waiting for transfers between devices, body(): lax.all_to_all(terms, 'expert', split_axis=0, concat_axis=0, tiled=True)  71 us
    dot_general x2, matrix products, body(): jnp.einsum('stc,std->scd', mine.reshape(devices, -1, CAP), all_normed.res...  11.7 us
    all_to_all x1, starting transfers between devices, body(): lax.all_to_all(terms, 'expert', split_axis=0, concat_axis=0, tiled=True)  9.7 us
    dot_general x2, matrix products, body(): up_value = jnp.dot(flat_rows, up_matrix, preferred_element_type=jnp.float32)  8.86 us
  transfers between devices with their start and end apart: 9, of which 3 were waited for; matrix products, arithmetic and copies ran while one was open for 4% of the time, Pallas kernels for 0%

commit v1 on v0

v1 whole, which is shorter than its diff:
```python
import functools
import math

import jax
import jax.numpy as jnp
from jax import lax
from jax.experimental import pallas as pl
from jax.experimental.pallas import tpu as pltpu
from jax.sharding import PartitionSpec as P

E_WIN = 2
CAP = 4
PIECES = 4
EPS = 1e-05
MESH = pl.DeviceIdType.MESH
F32, BF16 = jnp.float32, jnp.bfloat16


def bits(value, low, count):
    return lax.bitwise_and(lax.shift_right_logical(value, low), (1 << count) - 1)


def iota(shape, dim):
    return lax.broadcasted_iota(jnp.int32, shape, dim)


def one_hot(condition):
    return jnp.where(condition, 1.0, 0.0).astype(BF16)


def swap(rows, high, low, tail):
    to, frm = iota((rows, rows), 0), iota((rows, rows), 1)
    to_l, to_h = bits(to, tail + high, low), bits(to, tail, high)
    frm_h, frm_l = bits(frm, tail + low, high), bits(frm, tail, low)
    same = (bits(to, 0, tail) == bits(frm, 0, tail)) & (to_l == frm_l) & (to_h == frm_h)
    return one_hot(same)


def dot(a, b, **kw):
    return jnp.dot(a, b, preferred_element_type=F32, **kw)


def dot_t(a, b):
    return lax.dot_general(a, b, (((1,), (1,)), ((), ())), preferred_element_type=F32)


def kernel(side, tokens, ids, gain, router, w_gate, w_up, w_down, out,
           stream, normed, ids_all, gain_all, router_all, gate_all, up_all, down_all,
           pack_a, pack_b, unit_a, unit_b, ga, gb, ta, tb, sb, ra, rb, wa, wb, va, vb,
           own_sem, param_sem, param_send, dir_send, dir_recv, ring_send, ring_recv,
           back_send, back_recv, sum_send, sum_recv):
    lg = side.bit_length() - 1
    width = stream.shape[1]
    ca, cb = ga.shape[-1], gb.shape[-1]
    base_b = PIECES * ca
    s = lax.axis_index("section")
    me = lax.axis_index("expert")
    y, x = me // side, me % side
    expert = y // (side // E_WIN)
    bundle = side * CAP

    def at(yy, xx):
        return {"expert": yy * side + xx}

    other = {"section": 1 - s}
    params = ((gain, gain_all), (router, router_all), (w_gate, gate_all), (w_up, up_all), (w_down, down_all))

    def remote(src, dst, send, recv, device):
        return pltpu.make_async_remote_copy(src_ref=src, dst_ref=dst, send_sem=send, recv_sem=recv,
                                            device_id=device, device_id_type=MESH)

    token_copy = pltpu.make_async_copy(tokens.at[s], stream, own_sem)
    token_copy.start()
    pltpu.make_async_copy(ids.at[s], ids_all.at[s], param_sem.at[5, s]).start()
    for kind, (src, dst) in enumerate(params):
        pltpu.make_async_copy(src.at[0], dst.at[s], param_sem.at[kind, s]).start()

    barrier = pltpu.get_barrier_semaphore()
    pl.semaphore_signal(barrier, inc=1, device_id=other, device_id_type=MESH)
    for step in range(1, side):
        pl.semaphore_signal(barrier, inc=1, device_id=at(y, (x + step) % side), device_id_type=MESH)
        pl.semaphore_signal(barrier, inc=1, device_id=at((y + step) % side, x), device_id_type=MESH)
    pl.semaphore_wait(barrier, 2 * side - 1)

    sends = [remote(ids.at[1 - s], ids_all.at[s], param_send.at[5], param_sem.at[5, s], other)]
    for kind, (src, dst) in enumerate(params):
        sends.append(remote(src.at[0], dst.at[s], param_send.at[kind], param_sem.at[kind, s], other))
    for copy in sends:
        copy.start()

    def param_wait(kind, layer):
        src, dst = params[kind]
        pltpu.make_async_copy(src.at[0], dst.at[layer], param_sem.at[kind, layer]).wait()

    sb[...] = jnp.zeros_like(sb)
    token_copy.wait()

    def forward(piece):
        return 1 if piece < PIECES // 2 else -1

    def place(k):
        return x if k < PIECES else y

    def beside(k):
        go = forward(k % PIECES)
        return at(y, (x + go) % side) if k < PIECES else at((y + go) % side, x)

    def from_place(k, steps):
        return (place(k) + 8 * side - forward(k % PIECES) * steps) % side

    def gathered(k, layer, slot):
        return ga.at[layer, slot, k] if k < PIECES else gb.at[layer, slot, k - PIECES]

    def running(k, layer, step):
        return ra.at[layer, step, k] if k < PIECES else rb.at[layer, step, k - PIECES]

    streams = range(2 * PIECES)

    def one_layer(layer, carry):
        pltpu.make_async_copy(ids.at[s], ids_all.at[layer], param_sem.at[5, layer]).wait()
        param_wait(0, layer)
        param_wait(1, layer)
        values = stream[...].astype(F32)
        scale = lax.rsqrt(jnp.mean(values * values, axis=-1, keepdims=True) + EPS)
        normed[...] = (values * scale * gain_all[layer].astype(F32)).astype(BF16)
        id_block = ids_all[layer]
        rows8 = id_block.shape[0]
        lanes = iota((rows8, 128), 1)
        named = [id_block[:, k:k + 1] for k in range(2)]
        hot = [jnp.where(lanes == n, 1.0, 0.0) for n in named]
        earlier = jnp.where(iota((rows8, rows8), 0) > iota((rows8, rows8), 1), 1.0, 0.0)
        before = dot(earlier.astype(BF16), (hot[0] + hot[1]).astype(BF16))
        code = [jnp.sum(h * before, axis=-1, keepdims=True) + n.astype(F32) * CAP
                for h, n in zip(hot, named)]
        lane_f = lanes.astype(F32)
        joint = sum(jnp.where(lane_f == c, 1.0, 0.0) for c in code).astype(BF16)
        r = iota((32, 128), 0)
        c = iota((32, 128), 1)
        code_a = bits(r, 4, 1) * CAP + bits(r, 0, 2)
        code_b = bits(r, 0, 3)
        pick_a = dot_t(one_hot(c == code_a), joint)
        pick_b = dot_t(one_hot(c == code_b), joint)
        rr = iota((32, rows8), 0)
        packed_a = jnp.zeros((32, ca), F32)
        packed_b = jnp.zeros((32, cb), F32)
        for q in range(PIECES):
            mine_a = jnp.where(bits(rr, 2, 2) == q, pick_a, 0.0).astype(BF16)
            packed_a += dot(mine_a, normed[:, q * ca:(q + 1) * ca])
            mine_b = jnp.where(bits(rr, 3, 2) == q, pick_b, 0.0).astype(BF16)
            packed_b += dot(mine_b, normed[:, base_b + q * cb:base_b + (q + 1) * cb])
        pack_a[...] = packed_a.astype(BF16).reshape(E_WIN, PIECES * CAP, ca)
        pack_b[...] = packed_b.astype(BF16)
        unit_a[layer, y] = pack_a[expert]
        unit_b[layer, x] = pack_b[...]

        def direct_a(step):
            to = (y + step) % side
            return remote(pack_a.at[to // (side // E_WIN)], unit_a.at[layer, y], dir_send.at[0, step],
                          dir_recv.at[layer, 0, step], at(to, x))

        def direct_b(step):
            return remote(pack_b, unit_b.at[layer, x], dir_send.at[1, step],
                          dir_recv.at[layer, 1, step], at(y, (x + step) % side))

        for step in range(1, side):
            direct_a(step).start()
            direct_b(step).start()

        logits = dot_t(normed[...], router_all[layer])
        chosen = [jnp.sum(h[:, :logits.shape[1]] * logits, axis=-1, keepdims=True) for h in hot]
        gates = [jax.nn.sigmoid(chosen[0] - chosen[1]), jax.nn.sigmoid(chosen[1] - chosen[0])]

        for step in range(1, side):
            direct_a(step).wait()
        ga[layer, x] = dot(swap(side * 16, lg, 2, 2), unit_a[layer].reshape(side * 16, ca)).astype(BF16).reshape(
            PIECES, bundle, ca)

        def hop(k, step):
            slot = from_place(k, step)
            ref = gathered(k, layer, slot)
            return remote(ref, ref, ring_send.at[k], ring_recv.at[layer, k, step], beside(k))

        for k in range(PIECES):
            hop(k, 0).start()
        for step in range(1, side):
            direct_b(step).wait()
        gb[layer, y] = dot(swap(side * 32, lg, 3, 2), unit_b[layer].reshape(side * 32, cb)).astype(BF16).reshape(
            PIECES, 2 * bundle, cb)
        for k in range(PIECES, 2 * PIECES):
            hop(k, 0).start()

        def ring_step(step, c):
            for k in streams:
                hop(k, step - 1).wait()
                hop(k, step).start()
            return c

        lax.fori_loop(1, side - 1, ring_step, 0)
        for k in streams:
            hop(k, side - 2).wait()

        for kind in (2, 3, 4):
            param_wait(kind, layer)
        rows = side * bundle
        ff = gate_all.shape[-1]
        order = swap(rows, lg, lg, 2)

        def part_a(q, carry):
            g, u = carry
            lhs = ga[layer, :, q].reshape(rows, ca)
            at_rows = pl.ds(pl.multiple_of(q * ca, ca), ca)
            return g + dot(lhs, gate_all[layer, at_rows]), u + dot(lhs, up_all[layer, at_rows])

        def part_b(q, carry):
            g, u = carry
            lhs = gb[layer, :, q, pl.ds(pl.multiple_of(expert * bundle, bundle), bundle)].reshape(rows, cb)
            lhs = dot(order, lhs).astype(BF16)
            at_rows = pl.ds(pl.multiple_of(base_b + q * cb, cb), cb)
            return g + dot(lhs, gate_all[layer, at_rows]), u + dot(lhs, up_all[layer, at_rows])

        zero = jnp.zeros((rows, ff), F32)
        sums = lax.fori_loop(0, PIECES, part_a, (zero, zero))
        g, u = lax.fori_loop(0, PIECES, part_b, sums)
        hidden = (g * jax.nn.sigmoid(g) * u).astype(BF16)
        hidden_b = dot(order, hidden).astype(BF16)
        for q in range(PIECES):
            term = dot(hidden, down_all[layer, :, q * ca:(q + 1) * ca]).astype(BF16)
            ta[q] = term.reshape(side, bundle, ca)
            term = dot(hidden_b, down_all[layer, :, base_b + q * cb:base_b + (q + 1) * cb]).astype(BF16)
            tb[q] = term.reshape(side, bundle, cb)
        own_half = pl.ds(pl.multiple_of(expert * bundle, bundle), bundle)

        def pass_on(k, step):
            if step is None:
                src, step = (ta.at[k, from_place(k, 1)] if k < PIECES else sb.at[k - PIECES]), 0
            else:
                src = running(k, layer, step)
            return remote(src, running(k, layer, step + 1), sum_send.at[k], sum_recv.at[layer, k, step + 1],
                          beside(k))

        def add_own(k, step):
            slot = from_place(k, step + 1)
            if k < PIECES:
                ra[layer, step, k] = (ra[layer, step, k].astype(F32) + ta[k, slot].astype(F32)).astype(BF16)
            else:
                q = k - PIECES
                rb[layer, step, q, own_half] = (
                    rb[layer, step, q, own_half].astype(F32) + tb[q, slot].astype(F32)).astype(BF16)

        for k in streams:
            if k >= PIECES:
                sb[k - PIECES, own_half] = tb[k - PIECES, from_place(k, 1)]
            pass_on(k, None).start()
        for k in streams:
            pass_on(k, None).wait()
            add_own(k, 1)
            pass_on(k, 1).start()

        def sum_step(step, c):
            for k in streams:
                pass_on(k, step - 1).wait()
                add_own(k, step)
                pass_on(k, step).start()
            return c

        lax.fori_loop(2, side - 1, sum_step, 0)
        for k in streams:
            pass_on(k, side - 2).wait()
            add_own(k, side - 1)

        last = side - 1
        wa[...] = dot(swap(side * 16, 2, lg, 2), ra[layer, last].reshape(side * 16, ca)).astype(BF16).reshape(
            side, PIECES * CAP, ca)
        wb[...] = dot(swap(side * 32, 3, lg, 2), rb[layer, last].reshape(side * 32, cb)).astype(BF16).reshape(
            side, PIECES * 2 * CAP, cb)
        va[layer, y] = wa[y]
        vb[layer, x] = wb[x]

        def back_a(step):
            to = (y + step) % side
            return remote(wa.at[to], va.at[layer, y], back_send.at[0, step], back_recv.at[layer, 0, step], at(to, x))

        def back_b(step):
            to = (x + step) % side
            return remote(wb.at[to], vb.at[layer, x], back_send.at[1, step], back_recv.at[layer, 1, step], at(y, to))

        for step in range(1, side):
            back_a(step).start()
            back_b(step).start()
        for step in range(1, side):
            back_a(step).wait()
            back_b(step).wait()

        half = side // E_WIN
        out_a = jnp.concatenate(
            [sum(va[layer, n * half + j].astype(F32) for j in range(half)) for n in range(E_WIN)], axis=0)
        out_b = sum(vb[layer, j].astype(F32) for j in range(side))
        lane = iota((rows8, 32), 1)
        code_a = (bits(lane, 4, 1) * CAP + bits(lane, 0, 2)).astype(F32)
        code_b = bits(lane, 0, 3).astype(F32)
        weight_a = sum(jnp.where(code_a == c, g_, 0.0) for c, g_ in zip(code, gates))
        weight_b = sum(jnp.where(code_b == c, g_, 0.0) for c, g_ in zip(code, gates))
        for q in range(PIECES):
            for weight, which, value, begin, wide in (
                    (weight_a, bits(lane, 2, 2), out_a, q * ca, ca),
                    (weight_b, bits(lane, 3, 2), out_b, base_b + q * cb, cb)):
                moe = dot(jnp.where(which == q, weight, 0.0), value, precision=lax.Precision.HIGHEST)
                columns = slice(begin, begin + wide)
                stream[:, columns] = (stream[:, columns].astype(F32) + moe).astype(BF16)
        return carry

    lax.fori_loop(0, 2, one_layer, 0)
    out[0] = stream[...]
    for copy in sends:
        copy.wait_send()


def body(tokens, expert_ids, norm_gain, router, w_gate, w_up, w_down):
    side = math.isqrt(lax.axis_size("expert"))
    block, width = tokens.shape[1:]
    ff = w_gate.shape[-1]
    ca = width * 2 // 3 // PIECES
    cb = width // 3 // PIECES
    bundle = side * CAP
    ids = jnp.pad(expert_ids[0], ((0, 0), (0, 0), (0, 128 - expert_ids.shape[-1])))
    router_t = jnp.swapaxes(router, 1, 2)
    gain = norm_gain[:, None, :]
    dma = pltpu.SemaphoreType.DMA
    hbm = pl.BlockSpec(memory_space=pl.ANY)
    scratch = [
        pltpu.VMEM((block, width), BF16),
        pltpu.VMEM((block, width), BF16),
        pltpu.VMEM((2, block, 128), jnp.int32),
        pltpu.VMEM((2, 1, width), BF16),
        pltpu.VMEM((2, router.shape[-1], width), BF16),
        pltpu.VMEM((2, width, ff), BF16),
        pltpu.VMEM((2, width, ff), BF16),
        pltpu.VMEM((2, ff, width), BF16),
        pltpu.VMEM((E_WIN, PIECES * CAP, ca), BF16),
        pltpu.VMEM((PIECES * E_WIN * CAP, cb), BF16),
        pltpu.VMEM((2, side, PIECES * CAP, ca), BF16),
        pltpu.VMEM((2, side, PIECES * E_WIN * CAP, cb), BF16),
        pltpu.VMEM((2, side, PIECES, bundle, ca), BF16),
        pltpu.VMEM((2, side, PIECES, E_WIN * bundle, cb), BF16),
        pltpu.VMEM((PIECES, side, bundle, ca), BF16),
        pltpu.VMEM((PIECES, side, bundle, cb), BF16),
        pltpu.VMEM((PIECES, E_WIN * bundle, cb), BF16),
        pltpu.VMEM((2, side, PIECES, bundle, ca), BF16),
        pltpu.VMEM((2, side, PIECES, E_WIN * bundle, cb), BF16),
        pltpu.VMEM((side, PIECES * CAP, ca), BF16),
        pltpu.VMEM((side, PIECES * E_WIN * CAP, cb), BF16),
        pltpu.VMEM((2, side, PIECES * CAP, ca), BF16),
        pltpu.VMEM((2, side, PIECES * E_WIN * CAP, cb), BF16),
        dma,
        dma((6, 2)),
        dma((6,)),
        dma((2, side)),
        dma((2, 2, side)),
        dma((2 * PIECES,)),
        dma((2, 2 * PIECES, side)),
        dma((2, side)),
        dma((2, 2, side)),
        dma((2 * PIECES,)),
        dma((2, 2 * PIECES, side)),
    ]
    return pl.pallas_call(
        functools.partial(kernel, side),
        out_shape=jax.ShapeDtypeStruct((1, block, width), BF16),
        in_specs=[hbm] * 7,
        out_specs=pl.BlockSpec(memory_space=pltpu.VMEM),
        scratch_shapes=scratch,
        compiler_params=pltpu.CompilerParams(
            collective_id=0, has_side_effects=True, vmem_limit_bytes=60 * 1024 * 1024),
        name="moe_step",
    )(tokens, ids, gain, router_t, w_gate, w_up, w_down)


def solution(mesh):
    in_specs = (
        P(None, ("groups", "expert"), None),
        P("section", None, ("groups", "expert"), None),
        P("section", None),
        P("section", None, None),
        P("section", None, "expert"),
        P("section", None, "expert"),
        P("section", "expert", None),
    )
    out_specs = P("section", ("groups", "expert"), None)
    return jax.shard_map(body, mesh=mesh, in_specs=in_specs, out_specs=out_specs, check_vma=False)
```

time: 441 us -> 204 us (0.46)
  waiting for transfers between devices: 277 us -> 0 us
  Pallas kernels: 0 us -> 200 us
  blocking collectives: 79.5 us -> 0 us
  matrix products: 32.5 us -> 0 us
  between operations: 13.7 us -> 0.01 us
  starting transfers between devices: 11.7 us -> 0 us
  local copies, waits for them, and re-layouts: 14.5 us -> 2.91 us
  other arithmetic: 10.6 us -> 0 us
    all_gather x2 -> x0, waiting for transfers between devices: 206 us -> none  [side_by_side(): lax.all_gather(both, axis, axis=dim, tiled=True)]
    pallas_call x0 -> x1, Pallas kernels: none -> 200 us  [body(): pl.pallas_call(functools.partial(kernel, side), out_shape=jax.ShapeDtypeS...]
    all_to_all x1 -> x0, blocking collectives: 79.5 us -> none  [body(): lax.all_to_all(terms, 'expert', split_axis=0, concat_axis=0, tiled=True)]
    all_to_all x1 -> x0, waiting for transfers between devices: 71 us -> none  [body(): lax.all_to_all(terms, 'expert', split_axis=0, concat_axis=0, tiled=True)]
    dot_general x12 -> x0, matrix products: 32.5 us -> none  [the longest x2 11.7 us: body(): jnp.einsum('stc,std->scd', mine.reshape(devices, -1, CAP), all_normed.res...]
    reshape x6 -> x0, local copies, waits for them, and re-layouts: 10.4 us -> none  [the longest x2 5.37 us: body(): terms = term.reshape(sources, count, width)]
    all_to_all x1 -> x0, starting transfers between devices: 9.7 us -> none  [body(): lax.all_to_all(terms, 'expert', split_axis=0, concat_axis=0, tiled=True)]
    reduce_sum x9 -> x0, other arithmetic: 4.79 us -> none  [the longest x2 2.87 us: body(): jnp.sum(returned.reshape(E_WIN, split, CAP, D).astype(jnp.float32), axis=1)]
  transfers between devices with their start and end apart: 9 -> 0, of which waited for: 3 -> 0; matrix products, arithmetic and copies ran while one was open for 4% -> 0% of each run, Pallas kernels for 0% -> 0%
where the time goes in v1:
time: 204 us; the launch traced here: 203 us
  Pallas kernels  200 us (98%)
  local copies, waits for them, and re-layouts  2.91 us (1%)
    pallas_call x1, Pallas kernels, body(): pl.pallas_call(functools.partial(kernel, side), out_shape=jax.ShapeDtypeS...  200 us

profile of v1, /device:TPU:514, one launch (start us, length us, event | category | flops | bytes accessed | tf_op | source)
XLA Modules:
  0.0 203.3 jit_solution(3886938532204530179)
XLA Ops:
  0.0 0.8 copy.8
  0.8 0.6 pad.4.ids
  1.4 200.4 %moe_step.1 = bf16[1,8,6144]{2,1,0:T(8,128)(2,1)} custom-call(bf16[2,8,6144]{2,1,0:T(8,128)(2,1)} %tokens.1, s32[2,8,128]{2,1,0:T(8,128)} %pad.4.ids, bf16[1,1,6144]{2,1,0:T(2,128)(2,1)} %bitcast.4, bf16[1,8,6144]{2,1,0:T(8,128)(2,1)} %bitcast.3, bf16[1,6144,256]{2,1,0:T(8,128)(2,1)} %w_gate.1, bf16[1,6144,256]{2,1,0:T(8,128)(2,1)} %w_up.1, ...), custom_call_target="tpu_custom_call" | custom-call | tf_op jit(solution)/shard_map/moe_step/pallas_call | solution.py:366
  201.8 1.5 copy.10

commit v2 on v1

--- a/solution.py
+++ b/solution.py
@@ -46,7 +46,7 @@
 
 def kernel(side, tokens, ids, gain, router, w_gate, w_up, w_down, out,
            stream, normed, ids_all, gain_all, router_all, gate_all, up_all, down_all,
-           pack_a, pack_b, unit_a, unit_b, ga, gb, ta, tb, sb, ra, rb, wa, wb, va, vb,
+           pack_a, pack_b, unit_a, unit_b, ga, gb, ta, tb, sb, ra, rb, fa, fb, wa, wb, va, vb,
            own_sem, param_sem, param_send, dir_send, dir_recv, ring_send, ring_recv,
            back_send, back_recv, sum_send, sum_recv):
     lg = side.bit_length() - 1
@@ -95,26 +95,25 @@
     sb[...] = jnp.zeros_like(sb)
     token_copy.wait()
 
-    def forward(piece):
-        return 1 if piece < PIECES // 2 else -1
+    half_way = side // 2
+
+    def hops(k, go):
+        return half_way if (k % PIECES < PIECES // 2) == (go > 0) else half_way - 1
 
     def place(k):
         return x if k < PIECES else y
 
-    def beside(k):
-        go = forward(k % PIECES)
-        return at(y, (x + go) % side) if k < PIECES else at((y + go) % side, x)
-
-    def from_place(k, steps):
-        return (place(k) + 8 * side - forward(k % PIECES) * steps) % side
-
-    def gathered(k, layer, slot):
-        return ga.at[layer, slot, k] if k < PIECES else gb.at[layer, slot, k - PIECES]
-
-    def running(k, layer, step):
-        return ra.at[layer, step, k] if k < PIECES else rb.at[layer, step, k - PIECES]
-
-    streams = range(2 * PIECES)
+    def beside(k, go):
+        return at(y, (x + side + go) % side) if k < PIECES else at((y + side + go) % side, x)
+
+    def shift(k, steps):
+        return (place(k) + side + steps) % side
+
+    order_of = [0, 2, 1, 3]
+    streams = [(q + base, go) for q in order_of for base in (0, PIECES) for go in (1, -1)]
+
+    def way(go):
+        return 0 if go > 0 else 1
 
     def one_layer(layer, carry):
         pltpu.make_async_copy(ids.at[s], ids_all.at[layer], param_sem.at[5, layer]).wait()
@@ -124,15 +123,17 @@
         scale = lax.rsqrt(jnp.mean(values * values, axis=-1, keepdims=True) + EPS)
         normed[...] = (values * scale * gain_all[layer].astype(F32)).astype(BF16)
         id_block = ids_all[layer]
-        rows8 = id_block.shape[0]
+        rows8 = id_block.shape[1]
+        eye = one_hot(iota((rows8, rows8), 0) == iota((rows8, rows8), 1))
+        id_block = dot_t(eye, id_block.astype(F32).astype(BF16))
         lanes = iota((rows8, 128), 1)
         named = [id_block[:, k:k + 1] for k in range(2)]
-        hot = [jnp.where(lanes == n, 1.0, 0.0) for n in named]
+        lane_f = lanes.astype(F32)
+        hot = [jnp.where(lane_f == n, 1.0, 0.0) for n in named]
         earlier = jnp.where(iota((rows8, rows8), 0) > iota((rows8, rows8), 1), 1.0, 0.0)
         before = dot(earlier.astype(BF16), (hot[0] + hot[1]).astype(BF16))
-        code = [jnp.sum(h * before, axis=-1, keepdims=True) + n.astype(F32) * CAP
+        code = [jnp.sum(h * before, axis=-1, keepdims=True) + n * CAP
                 for h, n in zip(hot, named)]
-        lane_f = lanes.astype(F32)
         joint = sum(jnp.where(lane_f == c, 1.0, 0.0) for c in code).astype(BF16)
         r = iota((32, 128), 0)
         c = iota((32, 128), 1)
@@ -175,103 +176,103 @@
         ga[layer, x] = dot(swap(side * 16, lg, 2, 2), unit_a[layer].reshape(side * 16, ca)).astype(BF16).reshape(
             PIECES, bundle, ca)
 
-        def hop(k, step):
-            slot = from_place(k, step)
-            ref = gathered(k, layer, slot)
-            return remote(ref, ref, ring_send.at[k], ring_recv.at[layer, k, step], beside(k))
+        def hop(k, go, step):
+            slot = shift(k, -go * step)
+            ref = ga.at[layer, slot, k] if k < PIECES else gb.at[layer, slot, k - PIECES]
+            return remote(ref, ref, ring_send.at[k, way(go)], ring_recv.at[layer, k, way(go), step], beside(k, go))
 
         for k in range(PIECES):
-            hop(k, 0).start()
+            for go in (1, -1):
+                hop(k, go, 0).start()
         for step in range(1, side):
             direct_b(step).wait()
         gb[layer, y] = dot(swap(side * 32, lg, 3, 2), unit_b[layer].reshape(side * 32, cb)).astype(BF16).reshape(
             PIECES, 2 * bundle, cb)
         for k in range(PIECES, 2 * PIECES):
-            hop(k, 0).start()
+            for go in (1, -1):
+                hop(k, go, 0).start()
 
         def ring_step(step, c):
-            for k in streams:
-                hop(k, step - 1).wait()
-                hop(k, step).start()
+            for k, go in streams:
+                hop(k, go, step - 1).wait()
+                hop(k, go, step).start()
             return c
 
-        lax.fori_loop(1, side - 1, ring_step, 0)
-        for k in streams:
-            hop(k, side - 2).wait()
+        lax.fori_loop(1, half_way - 1, ring_step, 0)
+        for k, go in streams:
+            hop(k, go, half_way - 2).wait()
+            if hops(k, go) == half_way:
+                hop(k, go, half_way - 1).start()
 
         for kind in (2, 3, 4):
             param_wait(kind, layer)
         rows = side * bundle
-        ff = gate_all.shape[-1]
         order = swap(rows, lg, lg, 2)
-
-        def part_a(q, carry):
-            g, u = carry
-            lhs = ga[layer, :, q].reshape(rows, ca)
-            at_rows = pl.ds(pl.multiple_of(q * ca, ca), ca)
-            return g + dot(lhs, gate_all[layer, at_rows]), u + dot(lhs, up_all[layer, at_rows])
-
-        def part_b(q, carry):
-            g, u = carry
-            lhs = gb[layer, :, q, pl.ds(pl.multiple_of(expert * bundle, bundle), bundle)].reshape(rows, cb)
-            lhs = dot(order, lhs).astype(BF16)
-            at_rows = pl.ds(pl.multiple_of(base_b + q * cb, cb), cb)
-            return g + dot(lhs, gate_all[layer, at_rows]), u + dot(lhs, up_all[layer, at_rows])
-
-        zero = jnp.zeros((rows, ff), F32)
-        sums = lax.fori_loop(0, PIECES, part_a, (zero, zero))
-        g, u = lax.fori_loop(0, PIECES, part_b, sums)
+        own_half = pl.ds(pl.multiple_of(expert * bundle, bundle), bundle)
+        g = u = None
+        for q in order_of:
+            for k in (q, q + PIECES):
+                for go in (1, -1):
+                    if hops(k, go) == half_way:
+                        hop(k, go, half_way - 1).wait()
+            lhs_a = ga[layer, :, q].reshape(rows, ca)
+            at_a = pl.ds(q * ca, ca)
+            lhs_b = dot(order, gb[layer, :, q, own_half].reshape(rows, cb)).astype(BF16)
+            at_b = pl.ds(base_b + q * cb, cb)
+            part_g = dot(lhs_a, gate_all[layer, at_a]) + dot(lhs_b, gate_all[layer, at_b])
+            part_u = dot(lhs_a, up_all[layer, at_a]) + dot(lhs_b, up_all[layer, at_b])
+            g, u = (part_g, part_u) if g is None else (g + part_g, u + part_u)
         hidden = (g * jax.nn.sigmoid(g) * u).astype(BF16)
         hidden_b = dot(order, hidden).astype(BF16)
-        for q in range(PIECES):
+
+        def pass_on(k, go, step):
+            if k < PIECES:
+                src = ta.at[k, shift(k, go * hops(k, go))] if step == 0 else ra.at[layer, step - 1, way(go), k]
+                dst = ra.at[layer, step, way(go), k]
+            else:
+                q = k - PIECES
+                src = sb.at[way(go), q] if step == 0 else rb.at[layer, step - 1, way(go), q]
+                dst = rb.at[layer, step, way(go), q]
+            return remote(src, dst, sum_send.at[k, way(go)], sum_recv.at[layer, k, way(go), step], beside(k, go))
+
+        def add_own(k, go, step):
+            slot = shift(k, go * (hops(k, go) - step))
+            if k < PIECES:
+                at_ = (layer, step - 1, way(go), k)
+                ra[at_] = (ra[at_].astype(F32) + ta[k, slot].astype(F32)).astype(BF16)
+            else:
+                at_ = (layer, step - 1, way(go), k - PIECES, own_half)
+                rb[at_] = (rb[at_].astype(F32) + tb[k - PIECES, slot].astype(F32)).astype(BF16)
+
+        for q in order_of:
             term = dot(hidden, down_all[layer, :, q * ca:(q + 1) * ca]).astype(BF16)
             ta[q] = term.reshape(side, bundle, ca)
+            for go in (1, -1):
+                pass_on(q, go, 0).start()
             term = dot(hidden_b, down_all[layer, :, base_b + q * cb:base_b + (q + 1) * cb]).astype(BF16)
             tb[q] = term.reshape(side, bundle, cb)
-        own_half = pl.ds(pl.multiple_of(expert * bundle, bundle), bundle)
-
-        def pass_on(k, step):
-            if step is None:
-                src, step = (ta.at[k, from_place(k, 1)] if k < PIECES else sb.at[k - PIECES]), 0
-            else:
-                src = running(k, layer, step)
-            return remote(src, running(k, layer, step + 1), sum_send.at[k], sum_recv.at[layer, k, step + 1],
-                          beside(k))
-
-        def add_own(k, step):
-            slot = from_place(k, step + 1)
-            if k < PIECES:
-                ra[layer, step, k] = (ra[layer, step, k].astype(F32) + ta[k, slot].astype(F32)).astype(BF16)
-            else:
-                q = k - PIECES
-                rb[layer, step, q, own_half] = (
-                    rb[layer, step, q, own_half].astype(F32) + tb[q, slot].astype(F32)).astype(BF16)
-
-        for k in streams:
-            if k >= PIECES:
-                sb[k - PIECES, own_half] = tb[k - PIECES, from_place(k, 1)]
-            pass_on(k, None).start()
-        for k in streams:
-            pass_on(k, None).wait()
-            add_own(k, 1)
-            pass_on(k, 1).start()
-
-        def sum_step(step, c):
-            for k in streams:
-                pass_on(k, step - 1).wait()
-                add_own(k, step)
-                pass_on(k, step).start()
-            return c
-
-        lax.fori_loop(2, side - 1, sum_step, 0)
-        for k in streams:
-            pass_on(k, side - 2).wait()
-            add_own(k, side - 1)
-
-        last = side - 1
-        wa[...] = dot(swap(side * 16, 2, lg, 2), ra[layer, last].reshape(side * 16, ca)).astype(BF16).reshape(
-            side, PIECES * CAP, ca)
-        wb[...] = dot(swap(side * 32, 3, lg, 2), rb[layer, last].reshape(side * 32, cb)).astype(BF16).reshape(
+            for go in (1, -1):
+                k = q + PIECES
+                sb[way(go), q, own_half] = tb[q, shift(k, go * hops(k, go))]
+                pass_on(k, go, 0).start()
+
+        for step in range(1, half_way + 1):
+            for k, go in streams:
+                if step <= hops(k, go):
+                    pass_on(k, go, step - 1).wait()
+                if step < hops(k, go):
+                    add_own(k, go, step)
+                    pass_on(k, go, step).start()
+
+        def arrived(k, ref, *at_):
+            return sum(ref[(layer, hops(k, go) - 1, way(go), k % PIECES) + at_].astype(F32) for go in (1, -1))
+
+        for q in range(PIECES):
+            fa[q] = (arrived(q, ra) + ta[q, x].astype(F32)).astype(BF16)
+            fb[q] = arrived(q + PIECES, rb).astype(BF16)
+            fb[q, own_half] = (arrived(q + PIECES, rb, own_half) + tb[q, y].astype(F32)).astype(BF16)
+        wa[...] = dot(swap(side * 16, 2, lg, 2), fa[...].reshape(side * 16, ca)).astype(BF16).reshape(side, PIECES * CAP, ca)
+        wb[...] = dot(swap(side * 32, 3, lg, 2), fb[...].reshape(side * 32, cb)).astype(BF16).reshape(
             side, PIECES * 2 * CAP, cb)
         va[layer, y] = wa[y]
         vb[layer, x] = wb[x]
@@ -322,7 +323,7 @@
     ca = width * 2 // 3 // PIECES
     cb = width // 3 // PIECES
     bundle = side * CAP
-    ids = jnp.pad(expert_ids[0], ((0, 0), (0, 0), (0, 128 - expert_ids.shape[-1])))
+    ids = jnp.swapaxes(expert_ids[0], 1, 2)
     router_t = jnp.swapaxes(router, 1, 2)
     gain = norm_gain[:, None, :]
     dma = pltpu.SemaphoreType.DMA
@@ -330,7 +331,7 @@
     scratch = [
         pltpu.VMEM((block, width), BF16),
         pltpu.VMEM((block, width), BF16),
-        pltpu.VMEM((2, block, 128), jnp.int32),
+        pltpu.VMEM((2, 2, block), jnp.int32),
         pltpu.VMEM((2, 1, width), BF16),
         pltpu.VMEM((2, router.shape[-1], width), BF16),
         pltpu.VMEM((2, width, ff), BF16),
@@ -344,9 +345,11 @@
         pltpu.VMEM((2, side, PIECES, E_WIN * bundle, cb), BF16),
         pltpu.VMEM((PIECES, side, bundle, ca), BF16),
         pltpu.VMEM((PIECES, side, bundle, cb), BF16),
+        pltpu.VMEM((2, PIECES, E_WIN * bundle, cb), BF16),
+        pltpu.VMEM((2, side // 2, 2, PIECES, bundle, ca), BF16),
+        pltpu.VMEM((2, side // 2, 2, PIECES, E_WIN * bundle, cb), BF16),
+        pltpu.VMEM((PIECES, bundle, ca), BF16),
         pltpu.VMEM((PIECES, E_WIN * bundle, cb), BF16),
-        pltpu.VMEM((2, side, PIECES, bundle, ca), BF16),
-        pltpu.VMEM((2, side, PIECES, E_WIN * bundle, cb), BF16),
         pltpu.VMEM((side, PIECES * CAP, ca), BF16),
         pltpu.VMEM((side, PIECES * E_WIN * CAP, cb), BF16),
         pltpu.VMEM((2, side, PIECES * CAP, ca), BF16),
@@ -356,12 +359,12 @@
         dma((6,)),
         dma((2, side)),
         dma((2, 2, side)),
-        dma((2 * PIECES,)),
-        dma((2, 2 * PIECES, side)),
+        dma((2 * PIECES, 2)),
+        dma((2, 2 * PIECES, 2, side // 2)),
         dma((2, side)),
         dma((2, 2, side)),
-        dma((2 * PIECES,)),
-        dma((2, 2 * PIECES, side)),
+        dma((2 * PIECES, 2)),
+        dma((2, 2 * PIECES, 2, side // 2)),
     ]
     return pl.pallas_call(
         functools.partial(kernel, side),

time: 204 us -> 158 us (0.77)
  Pallas kernels: 200 us -> 157 us
    pallas_call x1, Pallas kernels: 200 us -> 157 us  [body(): pl.pallas_call(functools.partial(kernel, side), out_shape=jax.ShapeDtypeS...]
where the time goes in v2:
time: 158 us
  Pallas kernels  157 us (99%)
    pallas_call x1, Pallas kernels, body(): pl.pallas_call(functools.partial(kernel, side), out_shape=jax.ShapeDtypeS...  157 us

profile of v2, /device:TPU:514, one launch (start us, length us, event | category | flops | bytes accessed | tf_op | source)
XLA Modules:
  0.0 158.1 jit_solution(4112540506638504344)
XLA Ops:
  0.0 156.5 %moe_step.1 = bf16[1,8,6144]{2,1,0:T(8,128)(2,1)} custom-call(bf16[2,8,6144]{2,1,0:T(8,128)(2,1)} %tokens.1, s32[2,2,8]{2,1,0:T(2,128)} %bitcast.7, bf16[1,1,6144]{2,1,0:T(2,128)(2,1)} %bitcast.6, bf16[1,8,6144]{2,1,0:T(8,128)(2,1)} %bitcast.5, bf16[1,6144,256]{2,1,0:T(8,128)(2,1)} %w_gate.1, bf16[1,6144,256]{2,1,0:T(8,128)(2,1)} %w_up.1, ...), custom_call_target="tpu_custom_call" | custom-call | tf_op jit(solution)/shard_map/moe_step/pallas_call | solution.py:369
  156.5 1.5 copy.9

commit v3 on v2

--- a/solution.py
+++ b/solution.py
@@ -11,6 +11,7 @@
 E_WIN = 2
 CAP = 4
 PIECES = 4
+WAVES = 2
 EPS = 1e-05
 MESH = pl.DeviceIdType.MESH
 F32, BF16 = jnp.float32, jnp.bfloat16
@@ -69,17 +70,19 @@
         return pltpu.make_async_remote_copy(src_ref=src, dst_ref=dst, send_sem=send, recv_sem=recv,
                                             device_id=device, device_id_type=MESH)
 
+    barrier = pltpu.get_barrier_semaphore()
+    pl.semaphore_signal(barrier, inc=1, device_id=other, device_id_type=MESH)
+    for step in range(1, side):
+        pl.semaphore_signal(barrier, inc=1, device_id=at(y, (x + step) % side), device_id_type=MESH)
+        pl.semaphore_signal(barrier, inc=1, device_id=at((y + step) % side, x), device_id_type=MESH)
     token_copy = pltpu.make_async_copy(tokens.at[s], stream, own_sem)
     token_copy.start()
     pltpu.make_async_copy(ids.at[s], ids_all.at[s], param_sem.at[5, s]).start()
     for kind, (src, dst) in enumerate(params):
         pltpu.make_async_copy(src.at[0], dst.at[s], param_sem.at[kind, s]).start()
 
-    barrier = pltpu.get_barrier_semaphore()
-    pl.semaphore_signal(barrier, inc=1, device_id=other, device_id_type=MESH)
-    for step in range(1, side):
-        pl.semaphore_signal(barrier, inc=1, device_id=at(y, (x + step) % side), device_id_type=MESH)
-        pl.semaphore_signal(barrier, inc=1, device_id=at((y + step) % side, x), device_id_type=MESH)
+    sb[...] = jnp.zeros_like(sb)
+    token_copy.wait()
     pl.semaphore_wait(barrier, 2 * side - 1)
 
     sends = [remote(ids.at[1 - s], ids_all.at[s], param_send.at[5], param_sem.at[5, s], other)]
@@ -92,13 +95,10 @@
         src, dst = params[kind]
         pltpu.make_async_copy(src.at[0], dst.at[layer], param_sem.at[kind, layer]).wait()
 
-    sb[...] = jnp.zeros_like(sb)
-    token_copy.wait()
-
     half_way = side // 2
 
     def hops(k, go):
-        return half_way if (k % PIECES < PIECES // 2) == (go > 0) else half_way - 1
+        return half_way if (k % 2 == 0) == (go > 0) else half_way - 1
 
     def place(k):
         return x if k < PIECES else y
@@ -109,8 +109,13 @@
     def shift(k, steps):
         return (place(k) + side + steps) % side
 
-    order_of = [0, 2, 1, 3]
-    streams = [(q + base, go) for q in order_of for base in (0, PIECES) for go in (1, -1)]
+    waves = range(WAVES)
+    per = PIECES // WAVES
+
+    def of_wave(w):
+        return [(q + base, go) for q in range(w * per, (w + 1) * per) for base in (0, PIECES) for go in (1, -1)]
+
+    far_first = sorted(range(1, side), key=lambda step: -min(step, side - step))
 
     def way(go):
         return 0 if go > 0 else 1
@@ -135,74 +140,74 @@
         code = [jnp.sum(h * before, axis=-1, keepdims=True) + n * CAP
                 for h, n in zip(hot, named)]
         joint = sum(jnp.where(lane_f == c, 1.0, 0.0) for c in code).astype(BF16)
-        r = iota((32, 128), 0)
-        c = iota((32, 128), 1)
-        code_a = bits(r, 4, 1) * CAP + bits(r, 0, 2)
-        code_b = bits(r, 0, 3)
-        pick_a = dot_t(one_hot(c == code_a), joint)
-        pick_b = dot_t(one_hot(c == code_b), joint)
-        rr = iota((32, rows8), 0)
-        packed_a = jnp.zeros((32, ca), F32)
-        packed_b = jnp.zeros((32, cb), F32)
-        for q in range(PIECES):
-            mine_a = jnp.where(bits(rr, 2, 2) == q, pick_a, 0.0).astype(BF16)
-            packed_a += dot(mine_a, normed[:, q * ca:(q + 1) * ca])
-            mine_b = jnp.where(bits(rr, 3, 2) == q, pick_b, 0.0).astype(BF16)
-            packed_b += dot(mine_b, normed[:, base_b + q * cb:base_b + (q + 1) * cb])
-        pack_a[...] = packed_a.astype(BF16).reshape(E_WIN, PIECES * CAP, ca)
-        pack_b[...] = packed_b.astype(BF16)
-        unit_a[layer, y] = pack_a[expert]
-        unit_b[layer, x] = pack_b[...]
-
-        def direct_a(step):
+        r = iota((16, 128), 0)
+        c = iota((16, 128), 1)
+        pick_a = dot_t(one_hot(c == bits(r, 3, 1) * CAP + bits(r, 0, 2)), joint)
+        pick_b = dot_t(one_hot(c == bits(r, 0, 3)), joint)
+        rr = iota((16, rows8), 0)
+        mine_a = [jnp.where(bits(rr, 2, 1) == q, pick_a, 0.0).astype(BF16) for q in range(per)]
+        mine_b = [jnp.where(bits(rr, 3, 1) == q, pick_b, 0.0).astype(BF16) for q in range(per)]
+
+        def direct_a(w, step):
             to = (y + step) % side
-            return remote(pack_a.at[to // (side // E_WIN)], unit_a.at[layer, y], dir_send.at[0, step],
-                          dir_recv.at[layer, 0, step], at(to, x))
-
-        def direct_b(step):
-            return remote(pack_b, unit_b.at[layer, x], dir_send.at[1, step],
-                          dir_recv.at[layer, 1, step], at(y, (x + step) % side))
-
-        for step in range(1, side):
-            direct_a(step).start()
-            direct_b(step).start()
+            return remote(pack_a.at[w, to // (side // E_WIN)], unit_a.at[layer, w, y], dir_send.at[0, w, step],
+                          dir_recv.at[layer, 0, w, step], at(to, x))
+
+        def direct_b(w, step):
+            return remote(pack_b.at[w], unit_b.at[layer, w, x], dir_send.at[1, w, step],
+                          dir_recv.at[layer, 1, w, step], at(y, (x + step) % side))
+
+        for w in waves:
+            packed_a = sum(dot(mine_a[q], normed[:, (w * per + q) * ca:(w * per + q + 1) * ca]) for q in range(per))
+            pack_a[w] = packed_a.astype(BF16).reshape(E_WIN, per * CAP, ca)
+            packed_b = sum(dot(mine_b[q], normed[:, base_b + (w * per + q) * cb:base_b + (w * per + q + 1) * cb])
+                           for q in range(per))
+            pack_b[w] = packed_b.astype(BF16)
+            for step in far_first:
+                direct_a(w, step).start()
+                direct_b(w, step).start()
+            unit_a[layer, w, y] = pack_a[w, expert]
+            unit_b[layer, w, x] = pack_b[w]
 
         logits = dot_t(normed[...], router_all[layer])
         chosen = [jnp.sum(h[:, :logits.shape[1]] * logits, axis=-1, keepdims=True) for h in hot]
         gates = [jax.nn.sigmoid(chosen[0] - chosen[1]), jax.nn.sigmoid(chosen[1] - chosen[0])]
-
-        for step in range(1, side):
-            direct_a(step).wait()
-        ga[layer, x] = dot(swap(side * 16, lg, 2, 2), unit_a[layer].reshape(side * 16, ca)).astype(BF16).reshape(
-            PIECES, bundle, ca)
 
         def hop(k, go, step):
             slot = shift(k, -go * step)
             ref = ga.at[layer, slot, k] if k < PIECES else gb.at[layer, slot, k - PIECES]
             return remote(ref, ref, ring_send.at[k, way(go)], ring_recv.at[layer, k, way(go), step], beside(k, go))
 
-        for k in range(PIECES):
-            for go in (1, -1):
-                hop(k, go, 0).start()
-        for step in range(1, side):
-            direct_b(step).wait()
-        gb[layer, y] = dot(swap(side * 32, lg, 3, 2), unit_b[layer].reshape(side * 32, cb)).astype(BF16).reshape(
-            PIECES, 2 * bundle, cb)
-        for k in range(PIECES, 2 * PIECES):
-            for go in (1, -1):
-                hop(k, go, 0).start()
+        for w in waves:
+            now = pl.ds(w * per, per)
+            for step in range(1, side):
+                direct_a(w, step).wait()
+            ga[layer, x, now] = dot(swap(side * 8, lg, 1, 2), unit_a[layer, w].reshape(side * 8, ca)).astype(
+                BF16).reshape(per, bundle, ca)
+            for k, go in of_wave(w):
+                if k < PIECES:
+                    hop(k, go, 0).start()
+            for step in range(1, side):
+                direct_b(w, step).wait()
+            gb[layer, y, now] = dot(swap(side * 16, lg, 2, 2), unit_b[layer, w].reshape(side * 16, cb)).astype(
+                BF16).reshape(per, 2 * bundle, cb)
+            for k, go in of_wave(w):
+                if k >= PIECES:
+                    hop(k, go, 0).start()
 
         def ring_step(step, c):
-            for k, go in streams:
-                hop(k, go, step - 1).wait()
-                hop(k, go, step).start()
+            for w in waves:
+                for k, go in of_wave(w):
+                    hop(k, go, step - 1).wait()
+                    hop(k, go, step).start()
             return c
 
         lax.fori_loop(1, half_way - 1, ring_step, 0)
-        for k, go in streams:
-            hop(k, go, half_way - 2).wait()
-            if hops(k, go) == half_way:
-                hop(k, go, half_way - 1).start()
+        for w in waves:
+            for k, go in of_wave(w):
+                hop(k, go, half_way - 2).wait()
+                if hops(k, go) == half_way:
+                    hop(k, go, half_way - 1).start()
 
         for kind in (2, 3, 4):
             param_wait(kind, layer)
@@ -210,7 +215,7 @@
         order = swap(rows, lg, lg, 2)
         own_half = pl.ds(pl.multiple_of(expert * bundle, bundle), bundle)
         g = u = None
-        for q in order_of:
+        for q in range(PIECES):
             for k in (q, q + PIECES):
                 for go in (1, -1):
                     if hops(k, go) == half_way:
@@ -244,7 +249,7 @@
                 at_ = (layer, step - 1, way(go), k - PIECES, own_half)
                 rb[at_] = (rb[at_].astype(F32) + tb[k - PIECES, slot].astype(F32)).astype(BF16)
 
-        for q in order_of:
+        for q in range(PIECES):
             term = dot(hidden, down_all[layer, :, q * ca:(q + 1) * ca]).astype(BF16)
             ta[q] = term.reshape(side, bundle, ca)
             for go in (1, -1):
@@ -256,58 +261,65 @@
                 sb[way(go), q, own_half] = tb[q, shift(k, go * hops(k, go))]
                 pass_on(k, go, 0).start()
 
-        for step in range(1, half_way + 1):
-            for k, go in streams:
-                if step <= hops(k, go):
-                    pass_on(k, go, step - 1).wait()
-                if step < hops(k, go):
-                    add_own(k, go, step)
-                    pass_on(k, go, step).start()
-
         def arrived(k, ref, *at_):
             return sum(ref[(layer, hops(k, go) - 1, way(go), k % PIECES) + at_].astype(F32) for go in (1, -1))
 
-        for q in range(PIECES):
-            fa[q] = (arrived(q, ra) + ta[q, x].astype(F32)).astype(BF16)
-            fb[q] = arrived(q + PIECES, rb).astype(BF16)
-            fb[q, own_half] = (arrived(q + PIECES, rb, own_half) + tb[q, y].astype(F32)).astype(BF16)
-        wa[...] = dot(swap(side * 16, 2, lg, 2), fa[...].reshape(side * 16, ca)).astype(BF16).reshape(side, PIECES * CAP, ca)
-        wb[...] = dot(swap(side * 32, 3, lg, 2), fb[...].reshape(side * 32, cb)).astype(BF16).reshape(
-            side, PIECES * 2 * CAP, cb)
-        va[layer, y] = wa[y]
-        vb[layer, x] = wb[x]
-
-        def back_a(step):
+        def back_a(w, step):
             to = (y + step) % side
-            return remote(wa.at[to], va.at[layer, y], back_send.at[0, step], back_recv.at[layer, 0, step], at(to, x))
-
-        def back_b(step):
+            return remote(wa.at[w, to], va.at[layer, w, y], back_send.at[0, w, step],
+                          back_recv.at[layer, 0, w, step], at(to, x))
+
+        def back_b(w, step):
             to = (x + step) % side
-            return remote(wb.at[to], vb.at[layer, x], back_send.at[1, step], back_recv.at[layer, 1, step], at(y, to))
-
-        for step in range(1, side):
-            back_a(step).start()
-            back_b(step).start()
-        for step in range(1, side):
-            back_a(step).wait()
-            back_b(step).wait()
+            return remote(wb.at[w, to], vb.at[layer, w, x], back_send.at[1, w, step],
+                          back_recv.at[layer, 1, w, step], at(y, to))
+
+        for step in range(1, half_way + 1):
+            for w in waves:
+                for k, go in of_wave(w):
+                    if step <= hops(k, go):
+                        pass_on(k, go, step - 1).wait()
+                    if step < hops(k, go):
+                        add_own(k, go, step)
+                        pass_on(k, go, step).start()
+                if step < half_way:
+                    continue
+                for q in range(w * per, (w + 1) * per):
+                    fa[q] = (arrived(q, ra) + ta[q, x].astype(F32)).astype(BF16)
+                    fb[q] = arrived(q + PIECES, rb).astype(BF16)
+                    fb[q, own_half] = (arrived(q + PIECES, rb, own_half) + tb[q, y].astype(F32)).astype(BF16)
+                now = pl.ds(w * per, per)
+                wa[w] = dot(swap(side * 8, 1, lg, 2), fa[now].reshape(side * 8, ca)).astype(BF16).reshape(
+                    side, per * CAP, ca)
+                wb[w] = dot(swap(side * 16, 2, lg, 2), fb[now].reshape(side * 16, cb)).astype(BF16).reshape(
+                    side, per * 2 * CAP, cb)
+                for step_ in far_first:
+                    back_a(w, step_).start()
+                    back_b(w, step_).start()
+                va[layer, w, y] = wa[w, y]
+                vb[layer, w, x] = wb[w, x]
 
         half = side // E_WIN
-        out_a = jnp.concatenate(
-            [sum(va[layer, n * half + j].astype(F32) for j in range(half)) for n in range(E_WIN)], axis=0)
-        out_b = sum(vb[layer, j].astype(F32) for j in range(side))
-        lane = iota((rows8, 32), 1)
-        code_a = (bits(lane, 4, 1) * CAP + bits(lane, 0, 2)).astype(F32)
+        lane = iota((rows8, 16), 1)
+        code_a = (bits(lane, 3, 1) * CAP + bits(lane, 0, 2)).astype(F32)
         code_b = bits(lane, 0, 3).astype(F32)
         weight_a = sum(jnp.where(code_a == c, g_, 0.0) for c, g_ in zip(code, gates))
         weight_b = sum(jnp.where(code_b == c, g_, 0.0) for c, g_ in zip(code, gates))
-        for q in range(PIECES):
-            for weight, which, value, begin, wide in (
-                    (weight_a, bits(lane, 2, 2), out_a, q * ca, ca),
-                    (weight_b, bits(lane, 3, 2), out_b, base_b + q * cb, cb)):
-                moe = dot(jnp.where(which == q, weight, 0.0), value, precision=lax.Precision.HIGHEST)
-                columns = slice(begin, begin + wide)
-                stream[:, columns] = (stream[:, columns].astype(F32) + moe).astype(BF16)
+        for w in waves:
+            for step in range(1, side):
+                back_a(w, step).wait()
+                back_b(w, step).wait()
+            out_a = jnp.concatenate(
+                [sum(va[layer, w, n * half + j].astype(F32) for j in range(half)) for n in range(E_WIN)], axis=0)
+            out_b = sum(vb[layer, w, j].astype(F32) for j in range(side))
+            for q in range(per):
+                piece = w * per + q
+                for weight, which, value, begin, wide in (
+                        (weight_a, bits(lane, 2, 1), out_a, piece * ca, ca),
+                        (weight_b, bits(lane, 3, 1), out_b, base_b + piece * cb, cb)):
+                    moe = dot(jnp.where(which == q, weight, 0.0), value, precision=lax.Precision.HIGHEST)
+                    columns = slice(begin, begin + wide)
+                    stream[:, columns] = (stream[:, columns].astype(F32) + moe).astype(BF16)
         return carry
 
     lax.fori_loop(0, 2, one_layer, 0)
@@ -323,6 +335,7 @@
     ca = width * 2 // 3 // PIECES
     cb = width // 3 // PIECES
     bundle = side * CAP
+    per = PIECES // WAVES
     ids = jnp.swapaxes(expert_ids[0], 1, 2)
     router_t = jnp.swapaxes(router, 1, 2)
     gain = norm_gain[:, None, :]
@@ -337,10 +350,10 @@
         pltpu.VMEM((2, width, ff), BF16),
         pltpu.VMEM((2, width, ff), BF16),
         pltpu.VMEM((2, ff, width), BF16),
-        pltpu.VMEM((E_WIN, PIECES * CAP, ca), BF16),
-        pltpu.VMEM((PIECES * E_WIN * CAP, cb), BF16),
-        pltpu.VMEM((2, side, PIECES * CAP, ca), BF16),
-        pltpu.VMEM((2, side, PIECES * E_WIN * CAP, cb), BF16),
+        pltpu.VMEM((WAVES, E_WIN, per * CAP, ca), BF16),
+        pltpu.VMEM((WAVES, per * E_WIN * CAP, cb), BF16),
+        pltpu.VMEM((2, WAVES, side, per * CAP, ca), BF16),
+        pltpu.VMEM((2, WAVES, side, per * E_WIN * CAP, cb), BF16),
         pltpu.VMEM((2, side, PIECES, bundle, ca), BF16),
         pltpu.VMEM((2, side, PIECES, E_WIN * bundle, cb), BF16),
         pltpu.VMEM((PIECES, side, bundle, ca), BF16),
@@ -350,19 +363,19 @@
         pltpu.VMEM((2, side // 2, 2, PIECES, E_WIN * bundle, cb), BF16),
         pltpu.VMEM((PIECES, bundle, ca), BF16),
         pltpu.VMEM((PIECES, E_WIN * bundle, cb), BF16),
-        pltpu.VMEM((side, PIECES * CAP, ca), BF16),
-        pltpu.VMEM((side, PIECES * E_WIN * CAP, cb), BF16),
-        pltpu.VMEM((2, side, PIECES * CAP, ca), BF16),
-        pltpu.VMEM((2, side, PIECES * E_WIN * CAP, cb), BF16),
+        pltpu.VMEM((WAVES, side, per * CAP, ca), BF16),
+        pltpu.VMEM((WAVES, side, per * E_WIN * CAP, cb), BF16),
+        pltpu.VMEM((2, WAVES, side, per * CAP, ca), BF16),
+        pltpu.VMEM((2, WAVES, side, per * E_WIN * CAP, cb), BF16),
         dma,
         dma((6, 2)),
         dma((6,)),
-        dma((2, side)),
-        dma((2, 2, side)),
+        dma((2, WAVES, side)),
+        dma((2, 2, WAVES, side)),
         dma((2 * PIECES, 2)),
         dma((2, 2 * PIECES, 2, side // 2)),
-        dma((2, side)),
-        dma((2, 2, side)),
+        dma((2, WAVES, side)),
+        dma((2, 2, WAVES, side)),
         dma((2 * PIECES, 2)),
         dma((2, 2 * PIECES, 2, side // 2)),
     ]

time: 158 us -> 150 us (0.949)
  Pallas kernels: 157 us -> 149 us
    pallas_call x1, Pallas kernels: 157 us -> 149 us  [body(): pl.pallas_call(functools.partial(kernel, side), out_shape=jax.ShapeDtypeS...]
where the time goes in v3:
time: 150 us
  Pallas kernels  149 us (99%)
  local copies, waits for them, and re-layouts  1.54 us (1%)
    pallas_call x1, Pallas kernels, body(): pl.pallas_call(functools.partial(kernel, side), out_shape=jax.ShapeDtypeS...  149 us

profile of v3, /device:TPU:514, one launch (start us, length us, event | category | flops | bytes accessed | tf_op | source)
XLA Modules:
  0.0 150.1 jit_solution(2405640632672252662)
XLA Ops:
  0.0 148.5 %moe_step.1 = bf16[1,8,6144]{2,1,0:T(8,128)(2,1)} custom-call(bf16[2,8,6144]{2,1,0:T(8,128)(2,1)} %tokens.1, s32[2,2,8]{2,1,0:T(2,128)} %bitcast.7, bf16[1,1,6144]{2,1,0:T(2,128)(2,1)} %bitcast.6, bf16[1,8,6144]{2,1,0:T(8,128)(2,1)} %bitcast.5, bf16[1,6144,256]{2,1,0:T(8,128)(2,1)} %w_gate.1, bf16[1,6144,256]{2,1,0:T(8,128)(2,1)} %w_up.1, ...), custom_call_target="tpu_custom_call" | custom-call | tf_op jit(solution)/shard_map/moe_step/pallas_call | solution.py:382
  148.5 1.5 %copy.9 = bf16[1,8,6144]{2,1,0:T(8,128)(2,1)} copy(bf16[1,8,6144]{2,1,0:T(8,128)(2,1)} %moe_step.1) | data formatting | bytes 196608

commit v4 on v3

v4 whole, which is shorter than its diff:
```python
import functools
import math

import jax
import jax.numpy as jnp
from jax import lax
from jax.experimental import pallas as pl
from jax.experimental.pallas import tpu as pltpu
from jax.sharding import PartitionSpec as P

E_WIN = 2
CAP = 4
PIECES = 4
WAVES = 2
EPS = 1e-05
MESH = pl.DeviceIdType.MESH
F32, BF16 = jnp.float32, jnp.bfloat16


def bits(value, low, count):
    return lax.bitwise_and(lax.shift_right_logical(value, low), (1 << count) - 1)


def iota(shape, dim):
    return lax.broadcasted_iota(jnp.int32, shape, dim)


def one_hot(condition):
    return jnp.where(condition, 1.0, 0.0).astype(BF16)


def swap(rows, high, low, tail):
    to, frm = iota((rows, rows), 0), iota((rows, rows), 1)
    to_l, to_h = bits(to, tail + high, low), bits(to, tail, high)
    frm_h, frm_l = bits(frm, tail + low, high), bits(frm, tail, low)
    same = (bits(to, 0, tail) == bits(frm, 0, tail)) & (to_l == frm_l) & (to_h == frm_h)
    return one_hot(same)


def dot(a, b, **kw):
    return jnp.dot(a, b, preferred_element_type=F32, **kw)


def dot_t(a, b):
    return lax.dot_general(a, b, (((1,), (1,)), ((), ())), preferred_element_type=F32)


def kernel(side, tokens, ids, gain, router, w_gate, w_up, w_down, out,
           stream, normed, ids_all, gain_all, router_all, pair_all, down_all,
           pack_a, pack_b, unit_a, unit_b, ga, gb, ta, tb, ra, rb, fa, fb, wa, wb, va, vb,
           own_sem, param_sem, param_send, dir_send, dir_recv, ring_send, ring_recv,
           back_send, back_recv, sum_send, sum_recv):
    lg = side.bit_length() - 1
    width = stream.shape[1]
    ca, cb = ga.shape[-1], gb.shape[-1]
    base_b = PIECES * ca
    s = lax.axis_index("section")
    me = lax.axis_index("expert")
    y, x = lax.div(me, side), lax.rem(me, side)
    expert = lax.div(y, side // E_WIN)
    bundle = side * CAP

    def at(yy, xx):
        return {"expert": yy * side + xx}

    other = {"section": 1 - s}
    ff = down_all.shape[1]
    params = (
        (gain, lambda n: gain_all.at[n]),
        (router, lambda n: router_all.at[n]),
        (w_gate, lambda n: pair_all.at[n, :, pl.ds(0, ff)]),
        (w_up, lambda n: pair_all.at[n, :, pl.ds(ff, ff)]),
        (w_down, lambda n: down_all.at[n]),
    )

    def remote(src, dst, send, recv, device):
        return pltpu.make_async_remote_copy(src_ref=src, dst_ref=dst, send_sem=send, recv_sem=recv,
                                            device_id=device, device_id_type=MESH)

    barrier = pltpu.get_barrier_semaphore()
    pl.semaphore_signal(barrier, inc=1, device_id=other, device_id_type=MESH)
    for step in range(1, side):
        pl.semaphore_signal(barrier, inc=1, device_id=at(y, (x + step) % side), device_id_type=MESH)
        pl.semaphore_signal(barrier, inc=1, device_id=at((y + step) % side, x), device_id_type=MESH)
    token_copy = pltpu.make_async_copy(tokens.at[s], stream, own_sem)
    token_copy.start()
    pltpu.make_async_copy(ids.at[s], ids_all.at[s], param_sem.at[5, s]).start()
    for kind, (src, dst) in enumerate(params):
        pltpu.make_async_copy(src.at[0], dst(s), param_sem.at[kind, s]).start()

    token_copy.wait()
    pl.semaphore_wait(barrier, 2 * side - 1)

    sends = [remote(ids.at[1 - s], ids_all.at[s], param_send.at[5], param_sem.at[5, s], other)]
    for kind, (src, dst) in enumerate(params):
        sends.append(remote(src.at[0], dst(s), param_send.at[kind], param_sem.at[kind, s], other))
    for copy in sends:
        copy.start()

    def param_wait(kind, layer):
        src, dst = params[kind]
        pltpu.make_async_copy(src.at[0], dst(layer), param_sem.at[kind, layer]).wait()

    half_way = side // 2
    half = side // E_WIN
    per = PIECES // WAVES
    lp = per.bit_length() - 1
    unit = per * E_WIN * CAP
    ways = [(kind, is_far) for kind in range(2) for is_far in (True, False)]

    def heading(q, is_far):
        turn = 1 - 2 * lax.rem(q, 2)
        return turn if is_far else -turn

    def hops(is_far):
        return half_way if is_far else half_way - 1

    def way(go):
        return lax.div(1 - go, 2)

    def wrapped(value):
        return lax.rem(value + side, side)

    def beside(kind, go):
        return at(wrapped(y + go), x) if kind else at(y, wrapped(x + go))

    def shift(kind, steps):
        return wrapped((y if kind else x) + steps)

    def reaches(part, go, first, last):
        hit = None
        for j in range(first, last + 1):
            same = lax.div(wrapped(y + go * j), half) == part
            hit = same if hit is None else jnp.logical_or(hit, same)
        return hit

    def parts(go, first, last):
        each = [reaches(part, go, first, last) for part in range(E_WIN)]
        return jnp.logical_and(*each), lax.div(wrapped(y + go * first), half)

    def rows_of(part):
        return pl.ds(pl.multiple_of(part * bundle, bundle), bundle)

    def columns_of(kind, q):
        wide = cb if kind else ca
        return pl.ds(pl.multiple_of(q * wide + (base_b if kind else 0), 128), wide)

    def loop(first, last, step):
        def run(i, carry):
            step(i)
            return carry
        lax.fori_loop(first, last, run, 0)

    def wait_all(like, *sems):
        for sem in sems:
            pltpu.make_async_copy(like, like, sem).wait()

    def begin(hop):
        make, out_, _ = hop
        if out_ is None:
            make(None).start()
            return
        pl.when(out_[0])(lambda: make(pl.ds(0, E_WIN * bundle)).start())
        pl.when(jnp.logical_not(out_[0]))(lambda: make(rows_of(out_[1])).start())

    def finish(hop):
        make, out_, in_ = hop
        if out_ is None:
            make(None).wait()
            return
        everything, one = pl.ds(0, E_WIN * bundle), pl.ds(0, bundle)
        for which, end in ((out_, "wait_send"), (in_, "wait_recv")):
            pl.when(which[0])(lambda end=end: getattr(make(everything), end)())
            pl.when(jnp.logical_not(which[0]))(lambda end=end: getattr(make(one), end)())

    def one_layer(layer, carry):
        pltpu.make_async_copy(ids.at[s], ids_all.at[layer], param_sem.at[5, layer]).wait()
        param_wait(0, layer)
        param_wait(1, layer)
        values = stream[...].astype(F32)
        scale = lax.rsqrt(jnp.mean(values * values, axis=-1, keepdims=True) + EPS)
        normed[...] = (values * scale * gain_all[layer].astype(F32)).astype(BF16)
        id_block = ids_all[layer]
        rows8 = id_block.shape[1]
        eye = one_hot(iota((rows8, rows8), 0) == iota((rows8, rows8), 1))
        id_block = dot_t(eye, id_block.astype(F32).astype(BF16))
        lanes = iota((rows8, 128), 1)
        named = [id_block[:, k:k + 1] for k in range(2)]
        lane_f = lanes.astype(F32)
        hot = [jnp.where(lane_f == n, 1.0, 0.0) for n in named]
        earlier = jnp.where(iota((rows8, rows8), 0) > iota((rows8, rows8), 1), 1.0, 0.0)
        before = dot(earlier.astype(BF16), (hot[0] + hot[1]).astype(BF16))
        code = [jnp.sum(h * before, axis=-1, keepdims=True) + n * CAP
                for h, n in zip(hot, named)]
        joint = sum(jnp.where(lane_f == c, 1.0, 0.0) for c in code).astype(BF16)
        r = iota((unit, 128), 0)
        c = iota((unit, 128), 1)
        pick_a = dot_t(one_hot(c == bits(r, 2 + lp, 1) * CAP + bits(r, 0, 2)), joint)
        pick_b = dot_t(one_hot(c == bits(r, 0, 3)), joint)
        rr = iota((unit, rows8), 0)
        mine_a = [jnp.where(bits(rr, 2, lp) == q, pick_a, 0.0).astype(BF16) for q in range(per)]
        mine_b = [jnp.where(bits(rr, 3, lp) == q, pick_b, 0.0).astype(BF16) for q in range(per)]

        def direct(w, step, kind):
            to_y, to_x = wrapped(y + step), wrapped(x + step)
            if kind:
                return remote(pack_b.at[w], unit_b.at[layer, w, x], dir_send.at[1, w],
                              dir_recv.at[1, w], at(y, to_x))
            return remote(pack_a.at[w, lax.div(to_y, half)], unit_a.at[layer, w, y], dir_send.at[0, w],
                          dir_recv.at[0, w], at(to_y, x))

        def pack(w):
            first = w * per
            packed_a = sum(dot(mine_a[q], normed[:, columns_of(0, first + q)]) for q in range(per))
            pack_a[w] = packed_a.astype(BF16).reshape(E_WIN, per * CAP, ca)
            packed_b = sum(dot(mine_b[q], normed[:, columns_of(1, first + q)]) for q in range(per))
            pack_b[w] = packed_b.astype(BF16)

            def send(i):
                for kind in range(2):
                    direct(w, 1 + lax.rem(i + half_way - 1, side - 1), kind).start()

            loop(0, side - 1, send)
            unit_a[layer, w, y] = pack_a[w, expert]
            unit_b[layer, w, x] = pack_b[w]

        loop(0, WAVES, pack)

        logits = dot_t(normed[...], router_all[layer])
        chosen = [jnp.sum(h[:, :logits.shape[1]] * logits, axis=-1, keepdims=True) for h in hot]
        gates = [jax.nn.sigmoid(chosen[0] - chosen[1]), jax.nn.sigmoid(chosen[1] - chosen[0])]

        def hop(kind, q, is_far, step):
            go = heading(q, is_far)
            slot = shift(kind, -go * step)
            k = kind * PIECES + q
            sems = (ring_send.at[k, way(go)], ring_recv.at[k, way(go), step])

            def make(rows):
                ref = gb.at[layer, slot, q, rows] if kind else ga.at[layer, slot, q]
                return remote(ref, ref, *sems, beside(kind, go))

            left = hops(is_far) - step
            return (make, parts(go, 1, left), parts(go, 0, left - 1)) if kind else (make, None, None)

        def spread(w):
            now = pl.ds(w * per, per)
            wait_all(unit_a.at[layer, w, pl.ds(0, side - 1)], dir_send.at[0, w], dir_recv.at[0, w])
            ga[layer, x, now] = dot(
                swap(side * per * CAP, lg, lp, 2), unit_a[layer, w].reshape(side * per * CAP, ca)).astype(
                    BF16).reshape(per, bundle, ca)

            def start(kind):
                def go_on(i):
                    for is_far in (True, False):
                        begin(hop(kind, w * per + i, is_far, 0))
                loop(0, per, go_on)

            start(0)
            wait_all(unit_b.at[layer, w, pl.ds(0, side - 1)], dir_send.at[1, w], dir_recv.at[1, w])
            gb[layer, y, now] = dot(
                swap(side * unit, lg, lp + 1, 2), unit_b[layer, w].reshape(side * unit, cb)).astype(BF16).reshape(
                    per, 2 * bundle, cb)
            start(1)

        loop(0, WAVES, spread)

        for step in range(1, half_way):
            def ring_step(q, step=step):
                for kind, is_far in ways:
                    finish(hop(kind, q, is_far, step - 1))
                    if step < hops(is_far):
                        begin(hop(kind, q, is_far, step))
            loop(0, PIECES, ring_step)

        for kind in (2, 3, 4):
            param_wait(kind, layer)
        rows = side * bundle
        order = swap(rows, lg, lg, 2)
        own_half = rows_of(expert)

        def products(q, both):
            for kind in range(2):
                finish(hop(kind, q, True, half_way - 1))
            lhs_a = ga[layer, :, q].reshape(rows, ca)
            lhs_b = dot(order, gb[layer, :, q, own_half].reshape(rows, cb)).astype(BF16)
            return both + dot(lhs_a, pair_all[layer, columns_of(0, q)]) + dot(lhs_b, pair_all[layer, columns_of(1, q)])

        both = lax.fori_loop(0, PIECES, products, jnp.zeros((rows, 2 * ff), F32))
        g, u = both[:, :ff], both[:, ff:]
        hidden = (g * jax.nn.sigmoid(g) * u).astype(BF16)
        hidden_b = dot(order, hidden).astype(BF16)

        def pass_on(kind, q, is_far, step):
            go = heading(q, is_far)
            slot = shift(kind, go * hops(is_far))
            k = kind * PIECES + q
            sems = (sum_send.at[k, way(go)], sum_recv.at[k, way(go), step])

            def make(rows):
                if kind:
                    src = tb.at[q, slot] if step == 0 else rb.at[layer, step - 1, way(go), q, rows]
                    return remote(src, rb.at[layer, step, way(go), q, rows], *sems, beside(kind, go))
                src = ta.at[q, slot] if step == 0 else ra.at[layer, step - 1, way(go), q]
                return remote(src, ra.at[layer, step, way(go), q], *sems, beside(kind, go))

            return (make, parts(-go, 0, step), parts(-go, 1, step + 1)) if kind else (make, None, None)

        def add_own(kind, q, is_far, step):
            go = heading(q, is_far)
            slot = shift(kind, go * (hops(is_far) - step))
            if not kind:
                at_ = (layer, step - 1, way(go), q)
                ra[at_] = (ra[at_].astype(F32) + ta[q, slot].astype(F32)).astype(BF16)
                return
            at_ = (layer, step - 1, way(go), q, own_half)
            came = reaches(expert, -go, 1, step)

            def add():
                rb[at_] = (rb[at_].astype(F32) + tb[q, slot].astype(F32)).astype(BF16)

            def put():
                rb[at_] = tb[q, slot]

            pl.when(came)(add)
            pl.when(jnp.logical_not(came))(put)

        def clear(q, is_far):
            go = heading(q, is_far)
            for part in range(E_WIN):
                def zero(part=part):
                    rb[layer, hops(is_far) - 1, way(go), q, rows_of(part)] = jnp.zeros((bundle, cb), BF16)
                pl.when(jnp.logical_not(reaches(part, -go, 1, hops(is_far))))(zero)

        def begin_own(q, is_far):
            pass_on(1, q, is_far, 0)[0](own_half).start()

        def terms(q):
            ta[q] = dot(hidden, down_all[layer, :, columns_of(0, q)]).astype(BF16).reshape(side, bundle, ca)
            for is_far in (True, False):
                begin(pass_on(0, q, is_far, 0))
            tb[q] = dot(hidden_b, down_all[layer, :, columns_of(1, q)]).astype(BF16).reshape(side, bundle, cb)
            for is_far in (True, False):
                begin_own(q, is_far)
                clear(q, is_far)

        loop(0, PIECES, terms)

        for step in range(1, half_way):
            def sum_step(q, step=step):
                for kind, is_far in ways:
                    finish(pass_on(kind, q, is_far, step - 1))
                    if step < hops(is_far):
                        add_own(kind, q, is_far, step)
                        begin(pass_on(kind, q, is_far, step))
            loop(0, PIECES, sum_step)

        def back(w, step):
            to_y, to_x = wrapped(y + step), wrapped(x + step)
            return (remote(wa.at[w, to_y], va.at[layer, w, y], back_send.at[0, w],
                           back_recv.at[0, w], at(to_y, x)),
                    remote(wb.at[w, to_x], vb.at[layer, w, x], back_send.at[1, w],
                           back_recv.at[1, w], at(y, to_x)))

        def arrived(ref, q, *at_):
            return sum(ref[(layer, hops(is_far) - 1, way(heading(q, is_far)), q) + at_].astype(F32)
                       for is_far in (True, False))

        def give_back(w):
            def last(i):
                q = w * per + i
                for kind in range(2):
                    finish(pass_on(kind, q, True, half_way - 1))
                fa[q] = (arrived(ra, q) + ta[q, x].astype(F32)).astype(BF16)
                fb[q] = arrived(rb, q).astype(BF16)
                fb[q, own_half] = (arrived(rb, q, own_half) + tb[q, y].astype(F32)).astype(BF16)

            loop(0, per, last)
            now = pl.ds(w * per, per)
            wa[w] = dot(swap(side * per * CAP, lp, lg, 2), fa[now].reshape(side * per * CAP, ca)).astype(
                BF16).reshape(side, per * CAP, ca)
            wb[w] = dot(swap(side * unit, lp + 1, lg, 2), fb[now].reshape(side * unit, cb)).astype(BF16).reshape(
                side, unit, cb)

            def send(i):
                for copy in back(w, 1 + lax.rem(i + half_way - 1, side - 1)):
                    copy.start()

            loop(0, side - 1, send)
            va[layer, w, y] = wa[w, y]
            vb[layer, w, x] = wb[w, x]

        loop(0, WAVES, give_back)

        lane = iota((rows8, unit), 1)
        code_a = (bits(lane, 2 + lp, 1) * CAP + bits(lane, 0, 2)).astype(F32)
        code_b = bits(lane, 0, 3).astype(F32)
        weight_a = sum(jnp.where(code_a == c, g_, 0.0) for c, g_ in zip(code, gates))
        weight_b = sum(jnp.where(code_b == c, g_, 0.0) for c, g_ in zip(code, gates))

        def add_up(w):
            wait_all(va.at[layer, w, pl.ds(0, side - 1)], back_send.at[0, w], back_recv.at[0, w])
            wait_all(vb.at[layer, w, pl.ds(0, side - 1)], back_send.at[1, w], back_recv.at[1, w])
            out_a = jnp.concatenate(
                [sum(va[layer, w, n * half + j].astype(F32) for j in range(half)) for n in range(E_WIN)], axis=0)
            out_b = sum(vb[layer, w, j].astype(F32) for j in range(side))
            for q in range(per):
                for weight, which, value, kind in ((weight_a, bits(lane, 2, lp), out_a, 0),
                                                   (weight_b, bits(lane, 3, lp), out_b, 1)):
                    moe = dot(jnp.where(which == q, weight, 0.0), value, precision=lax.Precision.HIGHEST)
                    columns = columns_of(kind, w * per + q)
                    stream[:, columns] = (stream[:, columns].astype(F32) + moe).astype(BF16)

        loop(0, WAVES, add_up)
        return carry

    lax.fori_loop(0, 2, one_layer, 0)
    out[0] = stream[...]
    for copy in sends:
        copy.wait_send()


def body(tokens, expert_ids, norm_gain, router, w_gate, w_up, w_down):
    side = math.isqrt(lax.axis_size("expert"))
    block, width = tokens.shape[1:]
    ff = w_gate.shape[-1]
    ca = width * 2 // 3 // PIECES
    cb = width // 3 // PIECES
    bundle = side * CAP
    per = PIECES // WAVES
    ids = jnp.swapaxes(expert_ids[0], 1, 2)
    router_t = jnp.swapaxes(router, 1, 2)
    gain = norm_gain[:, None, :]
    dma = pltpu.SemaphoreType.DMA
    hbm = pl.BlockSpec(memory_space=pl.ANY)
    scratch = [
        pltpu.VMEM((block, width), BF16),
        pltpu.VMEM((block, width), BF16),
        pltpu.VMEM((2, 2, block), jnp.int32),
        pltpu.VMEM((2, 1, width), BF16),
        pltpu.VMEM((2, router.shape[-1], width), BF16),
        pltpu.VMEM((2, width, 2 * ff), BF16),
        pltpu.VMEM((2, ff, width), BF16),
        pltpu.VMEM((WAVES, E_WIN, per * CAP, ca), BF16),
        pltpu.VMEM((WAVES, per * E_WIN * CAP, cb), BF16),
        pltpu.VMEM((2, WAVES, side, per * CAP, ca), BF16),
        pltpu.VMEM((2, WAVES, side, per * E_WIN * CAP, cb), BF16),
        pltpu.VMEM((2, side, PIECES, bundle, ca), BF16),
        pltpu.VMEM((2, side, PIECES, E_WIN * bundle, cb), BF16),
        pltpu.VMEM((PIECES, side, bundle, ca), BF16),
        pltpu.VMEM((PIECES, side, bundle, cb), BF16),
        pltpu.VMEM((2, side // 2, 2, PIECES, bundle, ca), BF16),
        pltpu.VMEM((2, side // 2, 2, PIECES, E_WIN * bundle, cb), BF16),
        pltpu.VMEM((PIECES, bundle, ca), BF16),
        pltpu.VMEM((PIECES, E_WIN * bundle, cb), BF16),
        pltpu.VMEM((WAVES, side, per * CAP, ca), BF16),
        pltpu.VMEM((WAVES, side, per * E_WIN * CAP, cb), BF16),
        pltpu.VMEM((2, WAVES, side, per * CAP, ca), BF16),
        pltpu.VMEM((2, WAVES, side, per * E_WIN * CAP, cb), BF16),
        dma,
        dma((6, 2)),
        dma((6,)),
        dma((2, WAVES)),
        dma((2, WAVES)),
        dma((2 * PIECES, 2)),
        dma((2 * PIECES, 2, side // 2)),
        dma((2, WAVES)),
        dma((2, WAVES)),
        dma((2 * PIECES, 2)),
        dma((2 * PIECES, 2, side // 2)),
    ]
    return pl.pallas_call(
        functools.partial(kernel, side),
        out_shape=jax.ShapeDtypeStruct((1, block, width), BF16),
        in_specs=[hbm] * 7,
        out_specs=pl.BlockSpec(memory_space=pltpu.VMEM),
        scratch_shapes=scratch,
        compiler_params=pltpu.CompilerParams(
            collective_id=0, has_side_effects=True, vmem_limit_bytes=60 * 1024 * 1024),
        name="moe_step",
    )(tokens, ids, gain, router_t, w_gate, w_up, w_down)


def solution(mesh):
    in_specs = (
        P(None, ("groups", "expert"), None),
        P("section", None, ("groups", "expert"), None),
        P("section", None),
        P("section", None, None),
        P("section", None, "expert"),
        P("section", None, "expert"),
        P("section", "expert", None),
    )
    out_specs = P("section", ("groups", "expert"), None)
    return jax.shard_map(body, mesh=mesh, in_specs=in_specs, out_specs=out_specs, check_vma=False)
```

time: 150 us -> 146 us (0.973)
  Pallas kernels: 149 us -> 145 us
    pallas_call x1, Pallas kernels: 149 us -> 145 us  [body(): pl.pallas_call(functools.partial(kernel, side), out_shape=jax.ShapeDtypeS...]
where the time goes in v4:
time: 146 us
  Pallas kernels  145 us (99%)
  local copies, waits for them, and re-layouts  1.54 us (1%)
    pallas_call x1, Pallas kernels, body(): pl.pallas_call(functools.partial(kernel, side), out_shape=jax.ShapeDtypeS...  145 us

profile of v4, /device:TPU:514, one launch (start us, length us, event | category | flops | bytes accessed | tf_op | source)
XLA Modules:
  0.0 146.2 jit_solution(6742887715269657684)
XLA Ops:
  0.0 144.6 %moe_step.1 = bf16[1,8,6144]{2,1,0:T(8,128)(2,1)} custom-call(bf16[2,8,6144]{2,1,0:T(8,128)(2,1)} %tokens.1, s32[2,2,8]{2,1,0:T(2,128)} %bitcast.7, bf16[1,1,6144]{2,1,0:T(2,128)(2,1)} %bitcast.6, bf16[1,8,6144]{2,1,0:T(8,128)(2,1)} %bitcast.5, bf16[1,6144,256]{2,1,0:T(8,128)(2,1)} %w_gate.1, bf16[1,6144,256]{2,1,0:T(8,128)(2,1)} %w_up.1, ...), custom_call_target="tpu_custom_call" | custom-call | tf_op jit(solution)/shard_map/moe_step/pallas_call | solution.py:472
  144.6 1.5 %copy.9 = bf16[1,8,6144]{2,1,0:T(8,128)(2,1)} copy(bf16[1,8,6144]{2,1,0:T(8,128)(2,1)} %moe_step.1) | data formatting | bytes 196608

commit v5 on v4

--- a/solution.py
+++ b/solution.py
@@ -106,7 +106,7 @@
     per = PIECES // WAVES
     lp = per.bit_length() - 1
     unit = per * E_WIN * CAP
-    ways = [(kind, is_far) for kind in range(2) for is_far in (True, False)]
+    ways = [(kind, is_far) for is_far in (True, False) for kind in range(2)]
 
     def heading(q, is_far):
         turn = 1 - 2 * lax.rem(q, 2)
@@ -234,7 +234,7 @@
             go = heading(q, is_far)
             slot = shift(kind, -go * step)
             k = kind * PIECES + q
-            sems = (ring_send.at[k, way(go)], ring_recv.at[k, way(go), step])
+            sems = (ring_send.at[k, way(go)], ring_recv.at[k, step + (0 if is_far else half_way)])
 
             def make(rows):
                 ref = gb.at[layer, slot, q, rows] if kind else ga.at[layer, slot, q]
@@ -295,7 +295,7 @@
             go = heading(q, is_far)
             slot = shift(kind, go * hops(is_far))
             k = kind * PIECES + q
-            sems = (sum_send.at[k, way(go)], sum_recv.at[k, way(go), step])
+            sems = (sum_send.at[k, way(go)], sum_recv.at[k, step + (0 if is_far else half_way)])
 
             def make(rows):
                 if kind:
@@ -463,11 +463,11 @@
         dma((2, WAVES)),
         dma((2, WAVES)),
         dma((2 * PIECES, 2)),
-        dma((2 * PIECES, 2, side // 2)),
+        dma((2 * PIECES, side - 1)),
         dma((2, WAVES)),
         dma((2, WAVES)),
         dma((2 * PIECES, 2)),
-        dma((2 * PIECES, 2, side // 2)),
+        dma((2 * PIECES, side - 1)),
     ]
     return pl.pallas_call(
         functools.partial(kernel, side),

time: 146 us -> 146 us (level)
  no operation moved by 1% of the time
where the time goes in v5:
time: 146 us
  Pallas kernels  144 us (99%)
  local copies, waits for them, and re-layouts  1.54 us (1%)
    pallas_call x1, Pallas kernels, body(): pl.pallas_call(functools.partial(kernel, side), out_shape=jax.ShapeDtypeS...  144 us

profile of v5, /device:TPU:514, one launch (start us, length us, event | category | flops | bytes accessed | tf_op | source)
XLA Modules:
  0.0 146.0 jit_solution(12191294845080792135)
XLA Ops:
  0.0 144.5 %moe_step.1 = bf16[1,8,6144]{2,1,0:T(8,128)(2,1)} custom-call(bf16[2,8,6144]{2,1,0:T(8,128)(2,1)} %tokens.1, s32[2,2,8]{2,1,0:T(2,128)} %bitcast.7, bf16[1,1,6144]{2,1,0:T(2,128)(2,1)} %bitcast.6, bf16[1,8,6144]{2,1,0:T(8,128)(2,1)} %bitcast.5, bf16[1,6144,256]{2,1,0:T(8,128)(2,1)} %w_gate.1, bf16[1,6144,256]{2,1,0:T(8,128)(2,1)} %w_up.1, ...), custom_call_target="tpu_custom_call" | custom-call | tf_op jit(solution)/shard_map/moe_step/pallas_call | solution.py:472
  144.5 1.5 %copy.9 = bf16[1,8,6144]{2,1,0:T(8,128)(2,1)} copy(bf16[1,8,6144]{2,1,0:T(8,128)(2,1)} %moe_step.1) | data formatting | bytes 196608
